TPU v7x, 256 devices: a whole 4x4x8 slice. The times are simulated.
256 devices in a mesh: wide: 32 (over y, x, core), narrow: 8 (over z).
Axes of the slice: x: 4, y: 4, z: 8, core: 2. Of those that a mesh axis runs over, the one named last changes fastest.
Arguments:
- schur_matrix: bfloat16 [32, 8, 3, 1024, 1024], P('wide', 'narrow')
- face_inverse: bfloat16 [32, 8, 3, 8, 128, 128], P('wide', 'narrow')
- deluxe: bfloat16 [32, 8, 3, 8, 128, 128], P('wide', 'narrow')
- primal_weight: float32 [32, 8, 3, 8, 128], P('wide', 'narrow'), may hold values from 0.05 to 0.3
- coarse_group: float32 [32, 192, 192], P('wide', 'narrow')
- coarse_map: float32 [32, 192, 8], P('wide', 'narrow'), may hold values from -0.4375 to 0.4375
- coarse_top: float32 [256, 256], P('wide')
- load_vector: bfloat16 [32, 8, 3, 8, 128, 128], P('wide', 'narrow'), may hold values from -6 to 6
- previous: bfloat16 [32, 8, 3, 8, 128, 128], P('wide', 'narrow'), may hold values from -3 to 3
- slot_count: int32 [32, 8], P('wide', 'narrow'), may hold values from 1 to 3, as said below
- partner: int32 [32, 8, 3, 8], P('wide', 'narrow'), may hold values from -1 to 2, as said below
- face_size: int32 [32, 8, 3, 8], P('wide', 'narrow'), may hold values from 0 to 128, as said below
Outputs:
- solution: float32 [32, 8, 3, 8, 128, 128], P('wide', 'narrow')
- residual: float32 [32, 8, 3, 8, 128, 128], P('wide', 'narrow')
Inputs may be any that keep to these rules, and one draw needn't show every extreme that they name: Slots of a device below its slot_count hold subdomains; the others are empty. `face_size`: both sides of a face with a partner have the same size; faces of empty slots have size 0, all other faces at least 32.
All inputs are finite; a program needn't handle non-finite values.
Results may differ from a plain program's by a relative error of at most 0.00355.
The roundings to bfloat16 on the way count: a program that leaves them out, or rounds other values in their place, can miss the bound.
Values may be sent and summed in bfloat16 or wider, within the bound.
A program may use at most 128 MiB of HBM per device.

v0:
```python
import jax
import jax.numpy as jnp
from jax import lax
from jax.sharding import Mesh
from jax.sharding import PartitionSpec as P

ITERS = 2
WIDE = ("wide_0", "wide_1", "wide_2")
WIDE_NARROW = ("wide_0", "wide_1", "wide_2", "narrow")


precise = lax.Precision.HIGHEST


def with_halo(block, sides, width, periodic):
    for axis, dim in sides:
        count = lax.axis_size(axis)
        forward = [(i, i + 1) for i in range(count - 1)]
        if periodic:
            forward.append((count - 1, 0))
        backward = [(target, source) for source, target in forward]
        low = lax.ppermute(
            lax.slice_in_dim(block, block.shape[dim] - width, None, axis=dim), axis, forward
        )
        high = lax.ppermute(lax.slice_in_dim(block, 0, width, axis=dim), axis, backward)
        block = jnp.concatenate([low, block, high], axis=dim)
    return block


def over_axes(shard, axes):
    for axis in axes:
        shard = lax.psum(shard, axis)
    return shard


def in_order(pieces, dim):
    lengths = list(pieces.shape[1:])
    lengths[dim] *= pieces.shape[0]
    return jnp.moveaxis(pieces, 0, dim).reshape(lengths)


def copy_for_each(shard, axis):
    copies = jnp.broadcast_to(shard, (lax.axis_size(axis), *shard.shape))
    return lax.all_to_all(copies, axis, split_axis=0, concat_axis=0, tiled=True)


def gathered_copies(shard, axis, dim):
    return in_order(copy_for_each(shard, axis), dim)


def of_everyone(shard, axis):
    return copy_for_each(shard, axis).sum(axis=0)


def pick_partner(sources, partner):
    slot_total = sources.shape[1]
    chosen = partner[:, :, None] == jnp.arange(slot_total, dtype=jnp.int32)[None, None, :]
    spread = jnp.where(chosen[:, :, :, None, None], sources[None], jnp.zeros((), sources.dtype))
    return jnp.sum(spread, axis=2)


def face_sources(values, wide_got, narrow_got):
    return jnp.stack(
        [
            narrow_got[0],
            narrow_got[3],
            wide_got[0],
            wide_got[3],
            values[:, 5],
            values[:, 4],
            values[:, 7],
            values[:, 6],
        ],
        axis=0,
    )


def partner_full(values, partner):
    wide_got = with_halo(jnp.stack([values[:, 2], values[:, 3]], axis=0), ((WIDE, 0),), 1, True)
    narrow_got = with_halo(
        jnp.stack([values[:, 0], values[:, 1]], axis=0), (("narrow", 0),), 1, False
    )
    return pick_partner(face_sources(values, wide_got, narrow_got), partner)


def partner_half(values, partner):
    wide_got = with_halo(jnp.stack([values[:, 2], values[:, 3]], axis=0), ((WIDE, 0),), 1, True)
    narrow_got = with_halo(
        jnp.stack([values[:, 0], values[:, 1]], axis=0), (("narrow", 0),), 1, False
    )
    return pick_partner(face_sources(values, wide_got, narrow_got), partner)


def body(
    schur_matrix,
    face_inverse,
    deluxe,
    primal_weight,
    coarse_group,
    coarse_map,
    coarse_top,
    load_vector,
    previous,
    slot_count,
    partner,
    face_size,
):
    schur_matrix = schur_matrix[0, 0]
    face_inverse = face_inverse[0, 0]
    deluxe = deluxe[0, 0]
    primal_weight = primal_weight[0, 0]
    coarse_group = coarse_group[0]
    coarse_map = coarse_map[0]
    load_vector = load_vector[0, 0]
    previous = previous[0, 0]
    live_count = slot_count[0, 0]
    partner = partner[0, 0]
    face_size = face_size[0, 0]
    slot_total, face_total, face_width, columns = load_vector.shape
    block_order = schur_matrix.shape[1]
    slot_alive = jnp.arange(slot_total, dtype=jnp.int32)[:, None, None] < live_count
    inside = jnp.arange(face_width, dtype=jnp.int32)[None, None, :] < face_size[:, :, None]
    live_mask = jnp.where(jnp.logical_and(slot_alive, inside), 1.0, 0.0).astype(jnp.float32)[
        ..., None
    ]
    linked = (partner >= 0)[:, :, None, None]

    def global_inner(first_vec, second_vec, weights):
        return over_axes(jnp.sum(weights * first_vec * second_vec, axis=(0, 1, 2)), WIDE_NARROW)

    def operator(values):
        direction_half = values.astype(jnp.bfloat16)
        stacked = direction_half.reshape(slot_total, block_order, columns)
        result = jnp.einsum(
            "sij,sjr->sir", schur_matrix, stacked, preferred_element_type=jnp.float32
        )
        return live_mask * result.reshape(values.shape)

    def precondition(values):
        res_half = values.astype(jnp.bfloat16)
        scaled = live_mask * jnp.einsum(
            "sfkj,sfkr->sfjr", deluxe, res_half, preferred_element_type=jnp.float32
        )
        scaled_half = scaled.astype(jnp.bfloat16)
        local_part = jnp.einsum(
            "sfjk,sfkr->sfjr", face_inverse, scaled_half, preferred_element_type=jnp.float32
        )
        coarse_in = jnp.sum(primal_weight[..., None] * scaled, axis=2).reshape(
            slot_total * face_total, columns
        )
        group_vec = gathered_copies(coarse_in, "narrow", 0)
        group_part = jnp.dot(coarse_group, group_vec, precision=precise)
        restricted = of_everyone(jnp.dot(coarse_map.T, coarse_in, precision=precise), "narrow")
        everyone = gathered_copies(restricted, WIDE, 0)
        top_part = jnp.dot(coarse_top, everyone, precision=precise)
        coarse_out = group_part + jnp.dot(coarse_map, top_part, precision=precise)
        correction = local_part + primal_weight[..., None] * coarse_out.reshape(
            slot_total, face_total, 1, columns
        )
        corr_half = (live_mask * correction).astype(jnp.bfloat16)
        weighted = live_mask * jnp.einsum(
            "sfjk,sfkr->sfjr", deluxe, corr_half, preferred_element_type=jnp.float32
        )
        assembled = weighted + partner_full(weighted, partner)
        return (assembled, weighted)

    def norm_of(values, weighted):
        return global_inner(values, weighted, 1.0)

    prev_full = previous.astype(jnp.float32)
    prev_partner = partner_half(previous, partner).astype(jnp.float32)
    averaged = live_mask * jnp.where(linked, 0.5 * (prev_full + prev_partner), prev_full)
    start_local = live_mask * load_vector.astype(jnp.float32) - operator(averaged)
    residual = start_local + partner_full(start_local, partner)
    solution = averaged
    precond, weighted = precondition(residual)
    precond_norm = norm_of(residual, weighted)
    direction = precond
    for iteration in range(ITERS):
        image_local = operator(direction)
        curvature = global_inner(direction, image_local, 1.0)
        image_full = image_local + partner_full(image_local, partner)
        step_size = precond_norm / curvature
        solution = solution + step_size * direction
        residual = residual - step_size * image_full
        if iteration + 1 < ITERS:
            precond, weighted = precondition(residual)
            next_norm = norm_of(residual, weighted)
            direction = precond + next_norm / precond_norm * direction
            precond_norm = next_norm
    return (solution[None, None], residual[None, None])


def solution(mesh):
    split = Mesh(
        mesh.devices.reshape(4, 4, 2, mesh.shape["narrow"]),
        ("wide_0", "wide_1", "wide_2", "narrow"),
    )
    placed = (
        P(WIDE, "narrow", None, None, None),
        P(WIDE, "narrow", None, None, None, None),
        P(WIDE, "narrow", None, None, None, None),
        P(WIDE, "narrow", None, None, None),
        P(WIDE, "narrow", None),
        P(WIDE, "narrow", None),
        P(WIDE, None),
        P(WIDE, "narrow", None, None, None, None),
        P(WIDE, "narrow", None, None, None, None),
        P(WIDE, "narrow"),
        P(WIDE, "narrow", None, None),
        P(WIDE, "narrow", None, None),
    )
    return jax.shard_map(
        body,
        mesh=split,
        in_specs=placed,
        out_specs=(
            P(WIDE, "narrow", None, None, None, None),
            P(WIDE, "narrow", None, None, None, None),
        ),
        check_vma=False,
    )
```

profile of v0, /device:TPU:1, one launch (start us, length us, event | category | flops | bytes accessed | tf_op | source)
XLA Modules:
  0.0 342.8 jit_solution(6494169909488068758)
XLA Ops:
  6.4 4.6 %collective-permute-start = (bf16[1,3,128,128]{3,2,1,0:T(8,128)(2,1)S(1)}, bf16[1,3,128,128]{3,2,1,0:T(8,128)(2,1)}, u32[]{:S(2)}, u32[]{:S(2)}) collective-permute-start(bf16[1,3,128,128]{3,2,1,0:T(8,128)(2,1)S(1)} %get-tuple-element.42), channel_id=1, source_target_pairs={{0,1},{1,2},{2,3},{3,4},{4,5},{5,6},{6,7},{8,9},{9,10},{10,11},{11... | collective-permute-start | bytes 294920 | tf_op jit(solution)/shard_map/ppermute | solution.py:22
  22.6 6.6 %fusion.23 = f32[3,1024,128]{1,2,0:T(8,128)} fusion(bf16[1,1,3,1024,1024]{4,3,2,1,0:T(8,128)(2,1)} %param.12, f32[3,1024,128]{1,2,0:T(8,128)S(1)} %copy.76, f32[3,1024,128]{1,2,0:T(8,128)} %copy.77, f32[3,1024]{1,0:T(4,128)S(1)} %copy-done.30, pred[3,1024]{1,0:T(4,128)(4,1)S(1)} %bitcast.434), kind=kOutput, calls=%fused_computation.50 | convolution fusion | flops 807272448 | bytes 11025408 | tf_op jit(solution)/shard_map/sij,sjr->sir/dot_general | solution.py:134
  36.3 4.2 %collective-permute-start.7 = (f32[1,3,128,128]{3,2,1,0:T(8,128)S(1)}, f32[1,3,128,128]{3,2,1,0:T(8,128)S(1)}, u32[]{:S(2)}, u32[]{:S(2)}) collective-permute-start(f32[1,3,128,128]{3,2,1,0:T(8,128)S(1)} %get-tuple-element.35), channel_id=1, source_target_pairs={{8,0},{16,8},{24,16},{32,24},{40,32},{48,40},{56,48},{64,56},{72,6... | collective-permute-start | bytes 589832 | tf_op jit(solution)/shard_map/ppermute | solution.py:25
  41.6 4.2 %collective-permute-done.6 = f32[1,3,128,128]{3,2,1,0:T(8,128)S(1)} collective-permute-done((f32[1,3,128,128]{3,2,1,0:T(8,128)S(1)}, f32[1,3,128,128]{3,2,1,0:T(8,128)S(1)}, u32[]{:S(2)}, u32[]{:S(2)}) %collective-permute-start.6) | collective-permute-done | bytes 196640 | tf_op jit(solution)/shard_map/ppermute | solution.py:22
  49.9 16.3 %all_to_all.30 = f32[8,8,128]{2,1,0:T(8,128)S(1)} all-to-all(f32[8,8,128]{2,1,0:T(8,128)S(1)} %broadcast_in_dim.163), channel_id=1, replica_groups=mesh['wide_0'=4,'wide_1'=4,'wide_2'=2,'narrow'=8] {'narrow'}, dimensions={0} | all-to-all | bytes 65536 | tf_op jit(solution)/shard_map/all_to_all | solution.py:44
  70.2 7.5 %all-to-all-done = f32[8,24,128]{2,1,0:T(8,128)S(1)} async-done(((f32[8,24,128]{2,1,0:T(8,128)}), f32[8,24,128]{2,1,0:T(8,128)S(1)}, u32[]{:S(2)}, u32[]{:S(2)}) %all-to-all-start) | async-done | bytes 98336 | tf_op jit(solution)/shard_map/all_to_all | solution.py:44
  78.3 13.6 %all-to-all-start.2 = ((f32[32,8,128]{2,1,0:T(8,128)}), f32[32,8,128]{2,1,0:T(8,128)S(1)}, u32[]{:S(2)}, u32[]{:S(2)}) async-start(f32[32,8,128]{2,1,0:T(8,128)} %broadcast_in_dim.164), calls=%async_computation.2 | async-start | bytes 262144 | tf_op jit(solution)/shard_map/all_to_all | solution.py:44
  92.1 7.5 %all-to-all-done.2 = f32[32,8,128]{2,1,0:T(8,128)S(1)} async-done(((f32[32,8,128]{2,1,0:T(8,128)}), f32[32,8,128]{2,1,0:T(8,128)S(1)}, u32[]{:S(2)}, u32[]{:S(2)}) %all-to-all-start.2) | async-done | bytes 131104 | tf_op jit(solution)/shard_map/all_to_all | solution.py:44
  109.2 3.8 %collective-permute-done.9 = f32[1,3,128,128]{3,2,1,0:T(8,128)S(1)} collective-permute-done((f32[1,3,128,128]{3,2,1,0:T(8,128)S(1)}, f32[1,3,128,128]{3,2,1,0:T(8,128)S(1)}, u32[]{:S(2)}, u32[]{:S(2)}) %collective-permute-start.9) | collective-permute-done | bytes 196640 | tf_op jit(solution)/shard_map/ppermute | solution.py:25
  116.6 3.4 fusion.26
  127.0 4.0 %collective-permute-start.12 = (f32[1,3,128,128]{3,2,1,0:T(8,128)}, f32[1,3,128,128]{3,2,1,0:T(8,128)}, u32[]{:S(2)}, u32[]{:S(2)}) collective-permute-start(f32[1,3,128,128]{3,2,1,0:T(8,128)} %get-tuple-element.30), channel_id=1, source_target_pairs={{0,1},{1,2},{2,3},{3,4},{4,5},{5,6},{6,7},{8,9},{9,10},{10,11},{11... | collective-permute-start | bytes 589832 | tf_op jit(solution)/shard_map/ppermute | solution.py:22
  132.3 5.4 %collective-permute-start.15 = (f32[1,3,128,128]{3,2,1,0:T(8,128)S(1)}, f32[1,3,128,128]{3,2,1,0:T(8,128)}, u32[]{:S(2)}, u32[]{:S(2)}) collective-permute-start(f32[1,3,128,128]{3,2,1,0:T(8,128)S(1)} %get-tuple-element.27), channel_id=1, source_target_pairs={{8,0},{16,8},{24,16},{32,24},{40,32},{48,40},{56,48},{64,56},{72,6... | collective-permute-start | bytes 589832 | tf_op jit(solution)/shard_map/ppermute | solution.py:25
  137.7 7.2 %all-reduce.2 = (f32[128]{0:T(128)S(1)}, f32[128]{0:T(128)S(1)}) all-reduce(f32[128]{0:T(128)S(1)} %get-tuple-element.26, f32[128]{0:T(128)S(1)} %get-tuple-element.14), channel_id=1, replica_groups=mesh['wide_0'=4,'wide_1'=4,'wide_2'=2,'narrow'=8] {'wide_0'}, use_global_device_ids=true, to_apply=%region_5.6 | all-reduce | flops 256 | bytes 2048 | tf_op jit(solution)/shard_map/psum | solution.py:32
  144.9 9.8 %all-reduce.1 = (f32[128]{0:T(128)S(1)}, f32[128]{0:T(128)S(1)}) all-reduce(f32[128]{0:T(128)S(1)} %get-tuple-element.6, f32[128]{0:T(128)S(1)} %get-tuple-element.7), channel_id=1, replica_groups=mesh['wide_0'=4,'wide_1'=4,'wide_2'=2,'narrow'=8] {'wide_1'}, use_global_device_ids=true, to_apply=%region_6.7 | all-reduce | flops 256 | bytes 2048 | tf_op jit(solution)/shard_map/psum | solution.py:32
  157.1 13.0 %all-reduce = (f32[128]{0:T(128)S(1)}, f32[128]{0:T(128)S(1)}) all-reduce(f32[128]{0:T(128)S(1)} %get-tuple-element.8, f32[128]{0:T(128)S(1)} %get-tuple-element.9), channel_id=1, replica_groups=mesh['wide_0'=4,'wide_1'=4,'wide_2'=2,'narrow'=8] {'narrow'}, use_global_device_ids=true, to_apply=%region_8.9 | all-reduce | flops 256 | bytes 2048 | tf_op jit(solution)/shard_map/psum | solution.py:32
  178.1 10.4 %all_to_all.31 = f32[8,8,128]{2,1,0:T(8,128)S(1)} all-to-all(f32[8,8,128]{2,1,0:T(8,128)S(1)} %broadcast_in_dim.168), channel_id=1, replica_groups=mesh['wide_0'=4,'wide_1'=4,'wide_2'=2,'narrow'=8] {'narrow'}, dimensions={0} | all-to-all | bytes 65536 | tf_op jit(solution)/shard_map/all_to_all | solution.py:44
  192.5 7.5 %all-to-all-done.3 = f32[8,24,128]{2,1,0:T(8,128)S(1)} async-done(((f32[8,24,128]{2,1,0:T(8,128)}), f32[8,24,128]{2,1,0:T(8,128)S(1)}, u32[]{:S(2)}, u32[]{:S(2)}) %all-to-all-start.3) | async-done | bytes 98336 | tf_op jit(solution)/shard_map/all_to_all | solution.py:44
  200.7 9.9 %all-to-all-start.5 = ((f32[32,8,128]{2,1,0:T(8,128)}), f32[32,8,128]{2,1,0:T(8,128)S(1)}, u32[]{:S(2)}, u32[]{:S(2)}) async-start(f32[32,8,128]{2,1,0:T(8,128)} %broadcast_in_dim.169), calls=%async_computation.5 | async-start | bytes 262144 | tf_op jit(solution)/shard_map/all_to_all | solution.py:44
  210.7 7.4 %all-to-all-done.5 = f32[32,8,128]{2,1,0:T(8,128)S(1)} async-done(((f32[32,8,128]{2,1,0:T(8,128)}), f32[32,8,128]{2,1,0:T(8,128)S(1)}, u32[]{:S(2)}, u32[]{:S(2)}) %all-to-all-start.5) | async-done | bytes 131104 | tf_op jit(solution)/shard_map/all_to_all | solution.py:44
  218.8 4.4 %multiply_reduce_fusion.1 = (f32[128]{0:T(128)}, f32[3,8,128,128]{3,2,1,0:T(8,128)}) fusion(f32[3,8,128,128]{3,2,1,0:T(8,128)} %copy-done.20, bf16[1,1,3,8,128,128]{5,4,3,2,1,0:T(8,128)(2,1)S(1)} %copy-done.25, f32[3,8,128]{2,1,0:T(8,128)S(1)} %fusion.32, bf16[3,8,128,128]{2,3,1,0:T(8,128)(2,1)S(1)} %get-tuple-element.46, f32[3,8,128]{2,1,0:T(8,128)S(1)} %bitcast.429, ...), kind=kOutput, calls=%fused_computation.39 | convolution fusion | flops 204078976 | bytes 5542400 | tf_op jit(solution)/shard_map/sfjk,sfkr->sfjr/dot_general | solution.py:161
  229.5 6.9 %psum.120 = f32[128]{0:T(128)S(1)} all-reduce(f32[128]{0:T(128)S(1)} %copy-done.38), channel_id=1, replica_groups=mesh['wide_0'=4,'wide_1'=4,'wide_2'=2,'narrow'=8] {'wide_0'}, use_global_device_ids=true, to_apply=%region_19.20 | all-reduce | flops 128 | bytes 1024 | tf_op jit(solution)/shard_map/psum | solution.py:32
  236.3 7.0 %psum.121 = f32[128]{0:T(128)S(1)} all-reduce(f32[128]{0:T(128)S(1)} %psum.120), channel_id=1, replica_groups=mesh['wide_0'=4,'wide_1'=4,'wide_2'=2,'narrow'=8] {'wide_1'}, use_global_device_ids=true, to_apply=%region_20.21 | all-reduce | flops 128 | bytes 1024 | tf_op jit(solution)/shard_map/psum | solution.py:32
  243.3 6.8 %psum.122 = f32[128]{0:T(128)S(1)} all-reduce(f32[128]{0:T(128)S(1)} %psum.121), channel_id=1, replica_groups=mesh['wide_0'=4,'wide_1'=4,'wide_2'=2,'narrow'=8] {'wide_2'}, use_global_device_ids=true, to_apply=%region_21.22 | all-reduce | flops 128 | bytes 1024 | tf_op jit(solution)/shard_map/psum | solution.py:32
  250.1 13.0 %psum.123 = f32[128]{0:T(128)S(1)} all-reduce(f32[128]{0:T(128)S(1)} %psum.122), channel_id=1, replica_groups=mesh['wide_0'=4,'wide_1'=4,'wide_2'=2,'narrow'=8] {'narrow'}, use_global_device_ids=true, to_apply=%region_22.23 | all-reduce | flops 128 | bytes 1024 | tf_op jit(solution)/shard_map/psum | solution.py:32
  263.2 4.4 %collective-permute-start.19 = (f32[1,3,128,128]{3,2,1,0:T(8,128)S(1)}, f32[1,3,128,128]{3,2,1,0:T(8,128)S(1)}, u32[]{:S(2)}, u32[]{:S(2)}) collective-permute-start(f32[1,3,128,128]{3,2,1,0:T(8,128)S(1)} %get-tuple-element.22), channel_id=1, source_target_pairs={{8,0},{16,8},{24,16},{32,24},{40,32},{48,40},{56,48},{64,56},{72,6... | collective-permute-start | bytes 589832 | tf_op jit(solution)/shard_map/ppermute | solution.py:25
  276.2 3.4 fusion.29
  285.8 6.7 %psum.124 = f32[128]{0:T(128)S(1)} all-reduce(f32[128]{0:T(128)S(1)} %get-tuple-element.10), channel_id=1, replica_groups=mesh['wide_0'=4,'wide_1'=4,'wide_2'=2,'narrow'=8] {'wide_0'}, use_global_device_ids=true, to_apply=%region_25.26 | all-reduce | flops 128 | bytes 1024 | tf_op jit(solution)/shard_map/psum | solution.py:32
  292.6 10.0 %psum.125 = f32[128]{0:T(128)S(1)} all-reduce(f32[128]{0:T(128)S(1)} %psum.124), channel_id=1, replica_groups=mesh['wide_0'=4,'wide_1'=4,'wide_2'=2,'narrow'=8] {'wide_1'}, use_global_device_ids=true, to_apply=%region_26.27 | all-reduce | flops 128 | bytes 1024 | tf_op jit(solution)/shard_map/psum | solution.py:32
  302.6 5.8 %psum.126 = f32[128]{0:T(128)S(1)} all-reduce(f32[128]{0:T(128)S(1)} %psum.125), channel_id=1, replica_groups=mesh['wide_0'=4,'wide_1'=4,'wide_2'=2,'narrow'=8] {'wide_2'}, use_global_device_ids=true, to_apply=%region_27.28 | all-reduce | flops 128 | bytes 1024 | tf_op jit(solution)/shard_map/psum | solution.py:32
  308.4 10.8 %psum.127 = f32[128]{0:T(128)S(1)} all-reduce(f32[128]{0:T(128)S(1)} %psum.126), channel_id=1, replica_groups=mesh['wide_0'=4,'wide_1'=4,'wide_2'=2,'narrow'=8] {'narrow'}, use_global_device_ids=true, to_apply=%region_28.29 | all-reduce | flops 128 | bytes 1024 | tf_op jit(solution)/shard_map/psum | solution.py:32
  321.7 4.0 %collective-permute-start.20 = (f32[1,3,128,128]{3,2,1,0:T(8,128)S(1)}, f32[1,3,128,128]{3,2,1,0:T(8,128)S(1)}, u32[]{:S(2)}, u32[]{:S(2)}) collective-permute-start(f32[1,3,128,128]{3,2,1,0:T(8,128)S(1)} %get-tuple-element.21), channel_id=1, source_target_pairs={{0,1},{1,2},{2,3},{3,4},{4,5},{5,6},{6,7},{8,9},{9,10},{10,11},{11... | collective-permute-start | bytes 589832 | tf_op jit(solution)/shard_map/ppermute | solution.py:22
  329.0 4.3 %collective-permute-start.23 = (f32[1,3,128,128]{3,2,1,0:T(8,128)S(1)}, f32[1,3,128,128]{3,2,1,0:T(8,128)S(1)}, u32[]{:S(2)}, u32[]{:S(2)}) collective-permute-start(f32[1,3,128,128]{3,2,1,0:T(8,128)S(1)} %get-tuple-element.18), channel_id=1, source_target_pairs={{8,0},{16,8},{24,16},{32,24},{40,32},{48,40},{56,48},{64,56},{72,6... | collective-permute-start | bytes 589832 | tf_op jit(solution)/shard_map/ppermute | solution.py:25
  (245 shorter events, 106.6 us)
Async XLA Ops:
  0.6 47.0 %copy-start = (bf16[1,1,3,8,128,128]{5,4,3,2,1,0:T(8,128)(2,1)S(1)}, bf16[1,1,3,8,128,128]{5,4,3,2,1,0:T(8,128)(2,1)}, u32[]{:S(2)}) copy-start(bf16[1,1,3,8,128,128]{5,4,3,2,1,0:T(8,128)(2,1)} %param.14) | copy-start | bytes 2359300
  1.8 17.7 %collective-permute-start.3 = (bf16[1,3,128,128]{3,2,1,0:T(8,128)(2,1)S(1)}, bf16[1,3,128,128]{3,2,1,0:T(8,128)(2,1)}, u32[]{:S(2)}, u32[]{:S(2)}) collective-permute-start(bf16[1,3,128,128]{3,2,1,0:T(8,128)(2,1)S(1)} %get-tuple-element.39), channel_id=1, source_target_pairs={{8,0},{16,8},{24,16},{32,24},{40,32},{48,40},{56,48},{64,56},{72,6... | collective-permute-start | bytes 294920 | tf_op jit(solution)/shard_map/ppermute | solution.py:25
  5.1 13.5 %collective-permute-start.2 = (bf16[1,3,128,128]{3,2,1,0:T(8,128)(2,1)S(1)}, bf16[1,3,128,128]{3,2,1,0:T(8,128)(2,1)}, u32[]{:S(2)}, u32[]{:S(2)}) collective-permute-start(bf16[1,3,128,128]{3,2,1,0:T(8,128)(2,1)S(1)} %get-tuple-element.40), channel_id=1, source_target_pairs={{0,8},{8,16},{16,24},{24,32},{32,40},{40,48},{48,56},{56,64},{64,7... | collective-permute-start | bytes 294920 | tf_op jit(solution)/shard_map/ppermute | solution.py:22
  5.1 12.6 %collective-permute-start.1 = (bf16[1,3,128,128]{3,2,1,0:T(8,128)(2,1)S(1)}, bf16[1,3,128,128]{3,2,1,0:T(8,128)(2,1)}, u32[]{:S(2)}, u32[]{:S(2)}) collective-permute-start(bf16[1,3,128,128]{3,2,1,0:T(8,128)(2,1)S(1)} %get-tuple-element.41), channel_id=1, source_target_pairs={{1,0},{2,1},{3,2},{4,3},{5,4},{6,5},{7,6},{9,8},{10,9},{11,10},{12... | collective-permute-start | bytes 294920 | tf_op jit(solution)/shard_map/ppermute | solution.py:25
  6.4 10.4 %collective-permute-start = (bf16[1,3,128,128]{3,2,1,0:T(8,128)(2,1)S(1)}, bf16[1,3,128,128]{3,2,1,0:T(8,128)(2,1)}, u32[]{:S(2)}, u32[]{:S(2)}) collective-permute-start(bf16[1,3,128,128]{3,2,1,0:T(8,128)(2,1)S(1)} %get-tuple-element.42), channel_id=1, source_target_pairs={{0,1},{1,2},{2,3},{3,4},{4,5},{5,6},{6,7},{8,9},{9,10},{10,11},{11... | collective-permute-start | bytes 294920 | tf_op jit(solution)/shard_map/ppermute | solution.py:22
  32.4 8.1 %collective-permute-start.4 = (f32[1,3,128,128]{3,2,1,0:T(8,128)S(1)}, f32[1,3,128,128]{3,2,1,0:T(8,128)S(1)}, u32[]{:S(2)}, u32[]{:S(2)}) collective-permute-start(f32[1,3,128,128]{3,2,1,0:T(8,128)S(1)} %get-tuple-element.38), channel_id=1, source_target_pairs={{0,1},{1,2},{2,3},{3,4},{4,5},{5,6},{6,7},{8,9},{9,10},{10,11},{11... | collective-permute-start | bytes 589832 | tf_op jit(solution)/shard_map/ppermute | solution.py:22
  35.0 6.6 %collective-permute-start.5 = (f32[1,3,128,128]{3,2,1,0:T(8,128)S(1)}, f32[1,3,128,128]{3,2,1,0:T(8,128)S(1)}, u32[]{:S(2)}, u32[]{:S(2)}) collective-permute-start(f32[1,3,128,128]{3,2,1,0:T(8,128)S(1)} %get-tuple-element.37), channel_id=1, source_target_pairs={{1,0},{2,1},{3,2},{4,3},{5,4},{6,5},{7,6},{9,8},{10,9},{11,10},{12... | collective-permute-start | bytes 589832 | tf_op jit(solution)/shard_map/ppermute | solution.py:25
  36.3 9.6 %collective-permute-start.7 = (f32[1,3,128,128]{3,2,1,0:T(8,128)S(1)}, f32[1,3,128,128]{3,2,1,0:T(8,128)S(1)}, u32[]{:S(2)}, u32[]{:S(2)}) collective-permute-start(f32[1,3,128,128]{3,2,1,0:T(8,128)S(1)} %get-tuple-element.35), channel_id=1, source_target_pairs={{8,0},{16,8},{24,16},{32,24},{40,32},{48,40},{56,48},{64,56},{72,6... | collective-permute-start | bytes 589832 | tf_op jit(solution)/shard_map/ppermute | solution.py:25
  40.5 5.3 %collective-permute-start.6 = (f32[1,3,128,128]{3,2,1,0:T(8,128)S(1)}, f32[1,3,128,128]{3,2,1,0:T(8,128)S(1)}, u32[]{:S(2)}, u32[]{:S(2)}) collective-permute-start(f32[1,3,128,128]{3,2,1,0:T(8,128)S(1)} %get-tuple-element.36), channel_id=1, source_target_pairs={{0,8},{8,16},{16,24},{24,32},{32,40},{40,48},{48,56},{56,64},{64,7... | collective-permute-start | bytes 589832 | tf_op jit(solution)/shard_map/ppermute | solution.py:22
  47.7 52.0 %copy-start.32 = (f32[8,256]{1,0:T(8,128)S(1)}, f32[8,256]{1,0:T(8,128)}, u32[]{:S(2)}) copy-start(f32[8,256]{1,0:T(8,128)} %param.18) | copy-start | bytes 24580
  47.7 52.6 %copy-start.25 = (bf16[1,1,3,8,128,128]{5,4,3,2,1,0:T(8,128)(2,1)S(1)}, bf16[1,1,3,8,128,128]{5,4,3,2,1,0:T(8,128)(2,1)}, u32[]{:S(2)}) copy-start(bf16[1,1,3,8,128,128]{5,4,3,2,1,0:T(8,128)(2,1)} %param.13) | copy-start | bytes 2359300
  66.8 10.9 %all-to-all-start = ((f32[8,24,128]{2,1,0:T(8,128)}), f32[8,24,128]{2,1,0:T(8,128)S(1)}, u32[]{:S(2)}, u32[]{:S(2)}) async-start(f32[8,24,128]{2,1,0:T(8,128)} %broadcast_in_dim.162), calls=%async_computation | async-start | bytes 196608 | tf_op jit(solution)/shard_map/all_to_all | solution.py:44
  78.3 21.3 %all-to-all-start.2 = ((f32[32,8,128]{2,1,0:T(8,128)}), f32[32,8,128]{2,1,0:T(8,128)S(1)}, u32[]{:S(2)}, u32[]{:S(2)}) async-start(f32[32,8,128]{2,1,0:T(8,128)} %broadcast_in_dim.164), calls=%async_computation.2 | async-start | bytes 262144 | tf_op jit(solution)/shard_map/all_to_all | solution.py:44
  102.8 6.3 %collective-permute-start.8 = (f32[1,3,128,128]{3,2,1,0:T(8,128)S(1)}, f32[1,3,128,128]{3,2,1,0:T(8,128)S(1)}, u32[]{:S(2)}, u32[]{:S(2)}) collective-permute-start(f32[1,3,128,128]{3,2,1,0:T(8,128)S(1)} %get-tuple-element.34), channel_id=1, source_target_pairs={{0,1},{1,2},{2,3},{3,4},{4,5},{5,6},{6,7},{8,9},{9,10},{10,11},{11... | collective-permute-start | bytes 589832 | tf_op jit(solution)/shard_map/ppermute | solution.py:22
  105.3 7.7 %collective-permute-start.9 = (f32[1,3,128,128]{3,2,1,0:T(8,128)S(1)}, f32[1,3,128,128]{3,2,1,0:T(8,128)S(1)}, u32[]{:S(2)}, u32[]{:S(2)}) collective-permute-start(f32[1,3,128,128]{3,2,1,0:T(8,128)S(1)} %get-tuple-element.33), channel_id=1, source_target_pairs={{1,0},{2,1},{3,2},{4,3},{5,4},{6,5},{7,6},{9,8},{10,9},{11,10},{12... | collective-permute-start | bytes 589832 | tf_op jit(solution)/shard_map/ppermute | solution.py:25
  106.6 6.4 %collective-permute-start.11 = (f32[1,3,128,128]{3,2,1,0:T(8,128)S(1)}, f32[1,3,128,128]{3,2,1,0:T(8,128)S(1)}, u32[]{:S(2)}, u32[]{:S(2)}) collective-permute-start(f32[1,3,128,128]{3,2,1,0:T(8,128)S(1)} %get-tuple-element.31), channel_id=1, source_target_pairs={{8,0},{16,8},{24,16},{32,24},{40,32},{48,40},{56,48},{64,56},{72,6... | collective-permute-start | bytes 589832 | tf_op jit(solution)/shard_map/ppermute | solution.py:25
  107.6 5.4 %collective-permute-start.10 = (f32[1,3,128,128]{3,2,1,0:T(8,128)S(1)}, f32[1,3,128,128]{3,2,1,0:T(8,128)S(1)}, u32[]{:S(2)}, u32[]{:S(2)}) collective-permute-start(f32[1,3,128,128]{3,2,1,0:T(8,128)S(1)} %get-tuple-element.32), channel_id=1, source_target_pairs={{0,8},{8,16},{16,24},{24,32},{32,40},{40,48},{48,56},{56,64},{64,7... | collective-permute-start | bytes 589832 | tf_op jit(solution)/shard_map/ppermute | solution.py:22
  127.0 43.1 %collective-permute-start.12 = (f32[1,3,128,128]{3,2,1,0:T(8,128)}, f32[1,3,128,128]{3,2,1,0:T(8,128)}, u32[]{:S(2)}, u32[]{:S(2)}) collective-permute-start(f32[1,3,128,128]{3,2,1,0:T(8,128)} %get-tuple-element.30), channel_id=1, source_target_pairs={{0,1},{1,2},{2,3},{3,4},{4,5},{5,6},{6,7},{8,9},{9,10},{10,11},{11... | collective-permute-start | bytes 589832 | tf_op jit(solution)/shard_map/ppermute | solution.py:22
  131.0 40.1 %collective-permute-start.13 = (f32[1,3,128,128]{3,2,1,0:T(8,128)}, f32[1,3,128,128]{3,2,1,0:T(8,128)}, u32[]{:S(2)}, u32[]{:S(2)}) collective-permute-start(f32[1,3,128,128]{3,2,1,0:T(8,128)} %get-tuple-element.29), channel_id=1, source_target_pairs={{1,0},{2,1},{3,2},{4,3},{5,4},{6,5},{7,6},{9,8},{10,9},{11,10},{12... | collective-permute-start | bytes 589832 | tf_op jit(solution)/shard_map/ppermute | solution.py:25
  132.3 40.7 %collective-permute-start.15 = (f32[1,3,128,128]{3,2,1,0:T(8,128)S(1)}, f32[1,3,128,128]{3,2,1,0:T(8,128)}, u32[]{:S(2)}, u32[]{:S(2)}) collective-permute-start(f32[1,3,128,128]{3,2,1,0:T(8,128)S(1)} %get-tuple-element.27), channel_id=1, source_target_pairs={{8,0},{16,8},{24,16},{32,24},{40,32},{48,40},{56,48},{64,56},{72,6... | collective-permute-start | bytes 589832 | tf_op jit(solution)/shard_map/ppermute | solution.py:25
  137.7 34.4 %collective-permute-start.14 = (f32[1,3,128,128]{3,2,1,0:T(8,128)}, f32[1,3,128,128]{3,2,1,0:T(8,128)}, u32[]{:S(2)}, u32[]{:S(2)}) collective-permute-start(f32[1,3,128,128]{3,2,1,0:T(8,128)} %get-tuple-element.28), channel_id=1, source_target_pairs={{0,8},{8,16},{16,24},{24,32},{32,40},{40,48},{48,56},{56,64},{64,7... | collective-permute-start | bytes 589832 | tf_op jit(solution)/shard_map/ppermute | solution.py:22
  189.2 10.9 %all-to-all-start.3 = ((f32[8,24,128]{2,1,0:T(8,128)}), f32[8,24,128]{2,1,0:T(8,128)S(1)}, u32[]{:S(2)}, u32[]{:S(2)}) async-start(f32[8,24,128]{2,1,0:T(8,128)} %broadcast_in_dim.167), calls=%async_computation.3 | async-start | bytes 196608 | tf_op jit(solution)/shard_map/all_to_all | solution.py:44
  200.7 17.5 %all-to-all-start.5 = ((f32[32,8,128]{2,1,0:T(8,128)}), f32[32,8,128]{2,1,0:T(8,128)S(1)}, u32[]{:S(2)}, u32[]{:S(2)}) async-start(f32[32,8,128]{2,1,0:T(8,128)} %broadcast_in_dim.169), calls=%async_computation.5 | async-start | bytes 262144 | tf_op jit(solution)/shard_map/all_to_all | solution.py:44
  223.2 53.0 %slice-start.2 = ((s8[6291456]{0:T(1024)(128)(4,1)}), s8[2097152]{0:T(1024)(128)(4,1)S(1)}, s32[]{:S(2)}) async-start(s8[6291456]{0:T(1024)(128)(4,1)} %bitcast.407), calls=%async_computation.8 | async-start | bytes 4194304
  225.3 42.7 %collective-permute-start.16 = (f32[1,3,128,128]{3,2,1,0:T(8,128)}, f32[1,3,128,128]{3,2,1,0:T(8,128)}, u32[]{:S(2)}, u32[]{:S(2)}) collective-permute-start(f32[1,3,128,128]{3,2,1,0:T(8,128)} %get-tuple-element.25), channel_id=1, source_target_pairs={{0,1},{1,2},{2,3},{3,4},{4,5},{5,6},{6,7},{8,9},{9,10},{10,11},{11... | collective-permute-start | bytes 589832 | tf_op jit(solution)/shard_map/ppermute | solution.py:22
  228.2 40.8 %collective-permute-start.17 = (f32[1,3,128,128]{3,2,1,0:T(8,128)S(1)}, f32[1,3,128,128]{3,2,1,0:T(8,128)}, u32[]{:S(2)}, u32[]{:S(2)}) collective-permute-start(f32[1,3,128,128]{3,2,1,0:T(8,128)S(1)} %get-tuple-element.24), channel_id=1, source_target_pairs={{1,0},{2,1},{3,2},{4,3},{5,4},{6,5},{7,6},{9,8},{10,9},{11,10},{12... | collective-permute-start | bytes 589832 | tf_op jit(solution)/shard_map/ppermute | solution.py:25
  263.2 8.1 %collective-permute-start.19 = (f32[1,3,128,128]{3,2,1,0:T(8,128)S(1)}, f32[1,3,128,128]{3,2,1,0:T(8,128)S(1)}, u32[]{:S(2)}, u32[]{:S(2)}) collective-permute-start(f32[1,3,128,128]{3,2,1,0:T(8,128)S(1)} %get-tuple-element.22), channel_id=1, source_target_pairs={{8,0},{16,8},{24,16},{32,24},{40,32},{48,40},{56,48},{64,56},{72,6... | collective-permute-start | bytes 589832 | tf_op jit(solution)/shard_map/ppermute | solution.py:25
  267.6 3.0 collective-permute-start.18
  320.4 14.5 %collective-permute-start.21 = (f32[1,3,128,128]{3,2,1,0:T(8,128)S(1)}, f32[1,3,128,128]{3,2,1,0:T(8,128)S(1)}, u32[]{:S(2)}, u32[]{:S(2)}) collective-permute-start(f32[1,3,128,128]{3,2,1,0:T(8,128)S(1)} %get-tuple-element.20), channel_id=1, source_target_pairs={{1,0},{2,1},{3,2},{4,3},{5,4},{6,5},{7,6},{9,8},{10,9},{11,10},{12... | collective-permute-start | bytes 589832 | tf_op jit(solution)/shard_map/ppermute | solution.py:25
  321.7 13.1 %collective-permute-start.20 = (f32[1,3,128,128]{3,2,1,0:T(8,128)S(1)}, f32[1,3,128,128]{3,2,1,0:T(8,128)S(1)}, u32[]{:S(2)}, u32[]{:S(2)}) collective-permute-start(f32[1,3,128,128]{3,2,1,0:T(8,128)S(1)} %get-tuple-element.21), channel_id=1, source_target_pairs={{0,1},{1,2},{2,3},{3,4},{4,5},{5,6},{6,7},{8,9},{9,10},{10,11},{11... | collective-permute-start | bytes 589832 | tf_op jit(solution)/shard_map/ppermute | solution.py:22
  329.0 9.3 %collective-permute-start.23 = (f32[1,3,128,128]{3,2,1,0:T(8,128)S(1)}, f32[1,3,128,128]{3,2,1,0:T(8,128)S(1)}, u32[]{:S(2)}, u32[]{:S(2)}) collective-permute-start(f32[1,3,128,128]{3,2,1,0:T(8,128)S(1)} %get-tuple-element.18), channel_id=1, source_target_pairs={{8,0},{16,8},{24,16},{32,24},{40,32},{48,40},{56,48},{64,56},{72,6... | collective-permute-start | bytes 589832 | tf_op jit(solution)/shard_map/ppermute | solution.py:25
  333.2 4.2 %collective-permute-start.22 = (f32[1,3,128,128]{3,2,1,0:T(8,128)S(1)}, f32[1,3,128,128]{3,2,1,0:T(8,128)S(1)}, u32[]{:S(2)}, u32[]{:S(2)}) collective-permute-start(f32[1,3,128,128]{3,2,1,0:T(8,128)S(1)} %get-tuple-element.19), channel_id=1, source_target_pairs={{0,8},{8,16},{16,24},{24,32},{32,40},{40,48},{48,56},{56,64},{64,7... | collective-permute-start | bytes 589832 | tf_op jit(solution)/shard_map/ppermute | solution.py:22
  (43 other events, 482.5 us)
where the time goes:
time: 347 us; the launch traced here: 343 us
  blocking collectives  126 us (36%)
  starting transfers between devices  84 us (24%)
  waiting for transfers between devices  44.2 us (13%)
  local copies, waits for them, and re-layouts  40.8 us (12%)
  matrix products  25.5 us (7%)
  other arithmetic  19.7 us (6%)
    psum x12, blocking collectives, over_axes(): shard = lax.psum(shard, axis)  99.5 us
    ppermute x12, starting transfers between devices, with_halo(): lax.ppermute(lax.slice_in_dim(block, 0, width, axis=dim), axis, backward)  30.2 us
    all_to_all x4, starting transfers between devices, copy_for_each(): return lax.all_to_all(copies, axis, split_axis=0, concat_axis=0, tiled=True)  30.1 us
    all_to_all x4, waiting for transfers between devices, copy_for_each(): return lax.all_to_all(copies, axis, split_axis=0, concat_axis=0, tiled=True)  29.9 us
    all_to_all x2, blocking collectives, copy_for_each(): return lax.all_to_all(copies, axis, split_axis=0, concat_axis=0, tiled=True)  26.7 us
    ppermute x12, starting transfers between devices, with_halo(): lax.ppermute(lax.slice_in_dim(block, block.shape[dim] - width, None, axis...  23.7 us
    unnamed x141, local copies, waits for them, and re-layouts  22.9 us
    dot_general x3, matrix products, operator(): jnp.einsum('sij,sjr->sir', schur_matrix, stacked, preferred_element_type=...  13.4 us
  transfers between devices with their start and end apart: 28, of which 12 were waited for; matrix products, arithmetic and copies ran while one was open for 5% of the time, Pallas kernels for 0%

commit v1 on v0

v1 whole, which is shorter than its diff:
```python
import functools

import jax
import jax.numpy as jnp
from jax import lax
from jax.experimental import pallas as pl
from jax.experimental.pallas import tpu as pltpu
from jax.sharding import PartitionSpec as P

ITERS = 2
SLOTS = 3
NF = 8
FW = 128
NB = NF * FW
MESH = pl.DeviceIdType.MESH
HIGH = lax.Precision.HIGHEST
F32 = jnp.float32
BF16 = jnp.bfloat16
EXCHANGES = 2 * ITERS + 1
REDUCES = 2 * ITERS - 1


def kernel(
    wide,
    narrow,
    schur_in,
    inverse_in,
    deluxe_in,
    weight_in,
    group_ref,
    map_ref,
    top_ref,
    load_in,
    previous_in,
    count_ref,
    partner_ref,
    size_ref,
    solution_out,
    residual_out,
    schur,
    inverse,
    deluxe,
    load,
    previous,
    turned,
    weight,
    sol,
    res,
    direc,
    image,
    weighted,
    local,
    half,
    scaled_half,
    coarse,
    got_half,
    got_0,
    got_1,
    got_2,
    got_3,
    got_4,
    vec_buf,
    part_buf,
    every_buf,
    plane_buf,
    line_buf,
    load_sem,
    half_send,
    half_recv,
    face_send,
    face_recv,
    vec_send,
    vec_recv,
    part_send,
    part_recv,
    every_send,
    every_recv,
    plane_send,
    plane_recv,
    line_send,
    line_recv,
    out_sem,
):
    got = (got_0, got_1, got_2, got_3, got_4)
    w = lax.axis_index("wide")
    n = lax.axis_index("narrow")

    loads = [
        pltpu.make_async_copy(previous_in, previous, load_sem.at[0]),
        pltpu.make_async_copy(deluxe_in, deluxe, load_sem.at[1]),
        pltpu.make_async_copy(schur_in, schur, load_sem.at[2]),
        pltpu.make_async_copy(load_in, load, load_sem.at[3]),
        pltpu.make_async_copy(inverse_in, inverse, load_sem.at[4]),
    ]
    for copy in loads:
        copy.start()

    barrier = pltpu.get_barrier_semaphore()

    def greet_wide(d, carry):
        pl.semaphore_signal(
            barrier, inc=1, device_id=(lax.rem(w + d, wide), n), device_id_type=MESH
        )
        return carry

    def greet_narrow(d, carry):
        pl.semaphore_signal(
            barrier, inc=1, device_id=(w, lax.rem(n + d, narrow)), device_id_type=MESH
        )
        return carry

    lax.fori_loop(1, wide, greet_wide, 0)
    lax.fori_loop(1, narrow, greet_narrow, 0)

    rows = lax.broadcasted_iota(jnp.int32, (FW, FW), 0)
    count = count_ref[0, 0]

    def inside(s, f):
        size = jnp.where(s < count, size_ref[s, f], 0)
        return rows < size

    def masked(s, f, values):
        return jnp.where(inside(s, f), values, 0.0)

    def picked(values, arrived, s, f):
        t = partner_ref[s, f]
        slot = jnp.maximum(t, 0)
        source = arrived[f, slot] if f < 4 else values[slot, f ^ 1]
        return jnp.where(t >= 0, source.astype(F32), 0.0)

    def face_copies(values, arrived, send, recv, s):
        return [
            pltpu.make_async_remote_copy(
                src_ref=values.at[s, f],
                dst_ref=arrived.at[to, s],
                send_sem=send.at[to],
                recv_sem=recv.at[to],
                device_id=device,
                device_id_type=MESH,
            )
            for f, to, device in (
                (1, 0, (w, lax.rem(n + 1, narrow))),
                (0, 1, (w, lax.rem(n + narrow - 1, narrow))),
                (3, 2, (lax.rem(w + 1, wide), n)),
                (2, 3, (lax.rem(w + wide - 1, wide), n)),
            )
        ]

    def send_faces(values, arrived, send, recv, s):
        up, down, right, left = face_copies(values, arrived, send, recv, s)

        @pl.when(n < narrow - 1)
        def _():
            up.start()

        @pl.when(n > 0)
        def _():
            down.start()

        right.start()
        left.start()

    def wait_bytes(ref, sem):
        pltpu.make_async_copy(ref, ref, sem).wait()

    def wait_faces(arrived, recv):
        @pl.when(n > 0)
        def _():
            wait_bytes(arrived.at[0], recv.at[0])

        @pl.when(n < narrow - 1)
        def _():
            wait_bytes(arrived.at[1], recv.at[1])

        wait_bytes(arrived.at[2], recv.at[2])
        wait_bytes(arrived.at[3], recv.at[3])

    def wait_sent(arrived, send):
        @pl.when(n < narrow - 1)
        def _():
            wait_bytes(arrived.at[0], send.at[0])

        @pl.when(n > 0)
        def _():
            wait_bytes(arrived.at[1], send.at[1])

        wait_bytes(arrived.at[2], send.at[2])
        wait_bytes(arrived.at[3], send.at[3])

    def spread_narrow(buf, send, recv):
        def one(d, carry):
            pltpu.make_async_remote_copy(
                src_ref=buf.at[n],
                dst_ref=buf.at[n],
                send_sem=send,
                recv_sem=recv,
                device_id=(w, lax.rem(n + d, narrow)),
                device_id_type=MESH,
            ).start()
            return carry

        lax.fori_loop(1, narrow, one, 0)

    def spread_wide(buf, send, recv):
        def one(d, carry):
            pltpu.make_async_remote_copy(
                src_ref=buf.at[w],
                dst_ref=buf.at[w],
                send_sem=send,
                recv_sem=recv,
                device_id=(lax.rem(w + d, wide), n),
                device_id_type=MESH,
            ).start()
            return carry

        lax.fori_loop(1, wide, one, 0)

    def wait_spread(buf, sem):
        wait_bytes(buf.at[pl.ds(0, buf.shape[0] - 1)], sem)

    def fold(product):
        return jnp.sum(product.reshape(FW // 8, 8, FW), axis=0)

    def reduce_start(k, first, second):
        plane_buf[k, w] = jnp.concatenate(
            [jnp.sum(first, axis=0, keepdims=True), jnp.sum(second, axis=0, keepdims=True)], axis=0
        )
        spread_wide(plane_buf.at[k], plane_send.at[k], plane_recv.at[k])

    def reduce_middle(k):
        wait_spread(plane_buf.at[k], plane_recv.at[k])
        line_buf[k, n] = jnp.sum(plane_buf[k], axis=0)
        spread_narrow(line_buf.at[k], line_send.at[k], line_recv.at[k])

    def reduce_end(k):
        wait_spread(line_buf.at[k], line_recv.at[k])
        total = jnp.sum(line_buf[k], axis=0)
        return total[0:1], total[1:2]

    def spread_weight(s, carry):
        for f in range(NF):
            row = weight_in[s, f : f + 1, :]
            column = jnp.broadcast_to(row, (FW, FW)).T
            weight[s, f] = masked(s, f, column)
        return carry

    lax.fori_loop(0, SLOTS, spread_weight, 0)
    loads[1].wait()

    def turn(s, carry):
        for f in range(NF):
            turned[s, f] = deluxe[s, f].T
        return carry

    lax.fori_loop(0, SLOTS, turn, 0)
    loads[0].wait()
    pl.semaphore_wait(barrier, wide + narrow - 2)

    for s in range(SLOTS):
        send_faces(previous, got_half, half_send, half_recv, s)
    wait_faces(got_half, half_recv)

    def average(s, carry):
        for f in range(NF):
            own = previous[s, f].astype(F32)
            across = picked(previous, got_half, s, f)
            mean = jnp.where(partner_ref[s, f] >= 0, 0.5 * (own + across), own)
            mean = masked(s, f, mean)
            sol[s, f] = mean
            half[s, pl.ds(f * FW, FW), :] = mean.astype(BF16)
        return carry

    lax.fori_loop(0, SLOTS, average, 0)
    loads[2].wait()
    loads[3].wait()

    def start_residual(s, carry):
        product = jnp.dot(schur[s], half[s], preferred_element_type=F32)
        for f in range(NF):
            image[s, f] = masked(
                s, f, load[s, f].astype(F32) - product[f * FW : (f + 1) * FW]
            )
        send_faces(image, got[0], face_send.at[0], face_recv.at[0], s)
        return carry

    lax.fori_loop(0, SLOTS, start_residual, 0)
    loads[4].wait()
    zero = jnp.zeros((8, FW), F32)

    def scaled_of(m, s, f, values):
        scaled = masked(
            s, f, jnp.dot(turned[s, f], values.astype(BF16), preferred_element_type=F32)
        )
        scaled_half[s, f] = scaled.astype(BF16)
        return jnp.sum(fold(weight[s, f] * scaled), axis=0, keepdims=True)

    def coarse_start(m):
        entering = vec_buf[m, n]
        part_buf[m, n] = lax.dot_general(
            map_ref[...], entering, (((0,), (0,)), ((), ())), precision=HIGH
        )
        spread_narrow(part_buf.at[m], part_send.at[m], part_recv.at[m])
        spread_narrow(vec_buf.at[m], vec_send.at[m], vec_recv.at[m])

    def local_parts():
        def one(s, carry):
            for f in range(NF):
                local[s, f] = masked(
                    s, f, jnp.dot(inverse[s, f], scaled_half[s, f], preferred_element_type=F32)
                )
            return carry

        lax.fori_loop(0, SLOTS, one, 0)

    def coarse_end(m):
        wait_spread(part_buf.at[m], part_recv.at[m])
        every_buf[m, w] = jnp.sum(part_buf[m], axis=0)
        spread_wide(every_buf.at[m], every_send.at[m], every_recv.at[m])
        wait_spread(vec_buf.at[m], vec_recv.at[m])
        group = jnp.dot(
            group_ref[...], vec_buf[m].reshape(narrow * SLOTS * NF, FW), precision=HIGH
        )
        wait_spread(every_buf.at[m], every_recv.at[m])
        top = jnp.dot(top_ref[...], every_buf[m].reshape(wide * 8, FW), precision=HIGH)
        coarse[...] = group + jnp.dot(map_ref[...], top, precision=HIGH)

    def weigh(e, send_now):
        def one(s, total):
            for f in range(NF):
                out = coarse[pl.ds(s * NF + f, 1), :]
                correction = (local[s, f] + weight[s, f] * out).astype(BF16)
                value = masked(
                    s, f, jnp.dot(deluxe[s, f], correction, preferred_element_type=F32)
                )
                weighted[s, f] = value
                total = total + fold(res[s, f] * value)
            if send_now:
                send_faces(weighted, got[e], face_send.at[e], face_recv.at[e], s)
            return total

        return lax.fori_loop(0, SLOTS, one, zero)

    def operate(e):
        def one(s, total):
            product = jnp.dot(schur[s], half[s], preferred_element_type=F32)
            for f in range(NF):
                value = masked(s, f, product[f * FW : (f + 1) * FW])
                image[s, f] = value
                total = total + fold(direc[s, f] * value)
            return total

        return lax.fori_loop(0, SLOTS, one, zero)

    def send_all(values, e):
        def one(s, carry):
            send_faces(values, got[e], face_send.at[e], face_recv.at[e], s)
            return carry

        lax.fori_loop(0, SLOTS, one, 0)

    wait_faces(got[0], face_recv.at[0])

    def first_residual(s, carry):
        primal = []
        for f in range(NF):
            value = image[s, f] + picked(image, got[0], s, f)
            res[s, f] = value
            primal.append(scaled_of(0, s, f, value))
        vec_buf[0, n, pl.ds(s * NF, NF), :] = jnp.concatenate(primal, axis=0)
        return carry

    lax.fori_loop(0, SLOTS, first_residual, 0)
    coarse_start(0)
    local_parts()
    coarse_end(0)
    norm_part = weigh(1, True)
    wait_faces(got[1], face_recv.at[1])

    def first_direction(s, carry):
        for f in range(NF):
            value = weighted[s, f] + picked(weighted, got[1], s, f)
            direc[s, f] = value
            half[s, pl.ds(f * FW, FW), :] = value.astype(BF16)
        return carry

    lax.fori_loop(0, SLOTS, first_direction, 0)
    wait_sent(got[0], face_send.at[0])
    curve_part = operate(2)
    reduce_start(0, norm_part, curve_part)
    send_all(image, 2)
    reduce_middle(0)
    wait_faces(got[2], face_recv.at[2])
    norm, curve = reduce_end(0)
    step = norm / curve

    def next_residual(s, carry):
        primal = []
        for f in range(NF):
            full = image[s, f] + picked(image, got[2], s, f)
            value = res[s, f] - step * full
            res[s, f] = value
            primal.append(scaled_of(1, s, f, value))
        vec_buf[1, n, pl.ds(s * NF, NF), :] = jnp.concatenate(primal, axis=0)
        return carry

    lax.fori_loop(0, SLOTS, next_residual, 0)
    coarse_start(1)
    local_parts()

    def next_solution(s, carry):
        for f in range(NF):
            sol[s, f] = sol[s, f] + step * direc[s, f]
        return carry

    lax.fori_loop(0, SLOTS, next_solution, 0)
    wait_sent(got[1], face_send.at[1])
    coarse_end(1)
    norm_part = weigh(3, False)
    reduce_start(1, norm_part, norm_part)
    send_all(weighted, 3)
    reduce_middle(1)
    wait_faces(got[3], face_recv.at[3])
    following, _ = reduce_end(1)
    ratio = following / norm

    def next_direction(s, carry):
        for f in range(NF):
            value = weighted[s, f] + picked(weighted, got[3], s, f)
            value = value + ratio * direc[s, f]
            direc[s, f] = value
            half[s, pl.ds(f * FW, FW), :] = value.astype(BF16)
        return carry

    lax.fori_loop(0, SLOTS, next_direction, 0)
    wait_sent(got[2], face_send.at[2])
    curve_part = operate(4)
    reduce_start(2, curve_part, curve_part)
    send_all(image, 4)
    reduce_middle(2)
    wait_faces(got[4], face_recv.at[4])

    def last_image(s, carry):
        for f in range(NF):
            local[s, f] = image[s, f] + picked(image, got[4], s, f)
        return carry

    lax.fori_loop(0, SLOTS, last_image, 0)
    curve, _ = reduce_end(2)
    step = following / curve
    outs = []
    for s in range(SLOTS):
        for f in range(NF):
            sol[s, f] = sol[s, f] + step * direc[s, f]
        outs.append(pltpu.make_async_copy(sol.at[s], solution_out.at[s], out_sem.at[0, s]))
        outs[-1].start()
        for f in range(NF):
            res[s, f] = res[s, f] - step * local[s, f]
        outs.append(pltpu.make_async_copy(res.at[s], residual_out.at[s], out_sem.at[1, s]))
        outs[-1].start()

    wait_sent(got_half, half_send)
    wait_sent(got[3], face_send.at[3])
    wait_sent(got[4], face_send.at[4])
    for m in range(ITERS):
        wait_spread(part_buf.at[m], part_send.at[m])
        wait_spread(vec_buf.at[m], vec_send.at[m])
        wait_spread(every_buf.at[m], every_send.at[m])
    for k in range(REDUCES):
        wait_spread(plane_buf.at[k], plane_send.at[k])
        wait_spread(line_buf.at[k], line_send.at[k])
    for copy in outs:
        copy.wait()


def solution(mesh):
    wide, narrow = mesh.shape["wide"], mesh.shape["narrow"]
    faces = (SLOTS, NF, FW, FW)
    dma = pltpu.SemaphoreType.DMA

    def body(
        schur_matrix,
        face_inverse,
        deluxe,
        primal_weight,
        coarse_group,
        coarse_map,
        coarse_top,
        load_vector,
        previous,
        slot_count,
        partner,
        face_size,
    ):
        far = pl.BlockSpec(memory_space=pl.ANY)
        near = pl.BlockSpec(memory_space=pltpu.VMEM)
        scalar = pl.BlockSpec(memory_space=pltpu.SMEM)
        sol, res = pl.pallas_call(
            functools.partial(kernel, wide, narrow),
            out_shape=[jax.ShapeDtypeStruct(faces, F32)] * 2,
            in_specs=[far, far, far, near, near, near, near, far, far, scalar, scalar, scalar],
            out_specs=[far, far],
            scratch_shapes=[
                pltpu.VMEM((SLOTS, NB, NB), BF16),
                pltpu.VMEM(faces, BF16),
                pltpu.VMEM(faces, BF16),
                pltpu.VMEM(faces, BF16),
                pltpu.VMEM(faces, BF16),
                pltpu.VMEM(faces, BF16),
                pltpu.VMEM(faces, F32),
                pltpu.VMEM(faces, F32),
                pltpu.VMEM(faces, F32),
                pltpu.VMEM(faces, F32),
                pltpu.VMEM(faces, F32),
                pltpu.VMEM(faces, F32),
                pltpu.VMEM(faces, F32),
                pltpu.VMEM((SLOTS, NB, FW), BF16),
                pltpu.VMEM(faces, BF16),
                pltpu.VMEM((SLOTS * NF, FW), F32),
                pltpu.VMEM((4, SLOTS, FW, FW), BF16),
                *[pltpu.VMEM((4, SLOTS, FW, FW), F32)] * EXCHANGES,
                pltpu.VMEM((ITERS, narrow, SLOTS * NF, FW), F32),
                pltpu.VMEM((ITERS, narrow, 8, FW), F32),
                pltpu.VMEM((ITERS, wide, 8, FW), F32),
                pltpu.VMEM((REDUCES, wide, 2, FW), F32),
                pltpu.VMEM((REDUCES, narrow, 2, FW), F32),
                dma((5,)),
                dma((4,)),
                dma((4,)),
                dma((EXCHANGES, 4)),
                dma((EXCHANGES, 4)),
                dma((ITERS,)),
                dma((ITERS,)),
                dma((ITERS,)),
                dma((ITERS,)),
                dma((ITERS,)),
                dma((ITERS,)),
                dma((REDUCES,)),
                dma((REDUCES,)),
                dma((REDUCES,)),
                dma((REDUCES,)),
                dma((2, SLOTS)),
            ],
            compiler_params=pltpu.CompilerParams(
                collective_id=0, has_side_effects=True, vmem_limit_bytes=60 * 1024 * 1024
            ),
        )(
            schur_matrix[0, 0],
            face_inverse[0, 0],
            deluxe[0, 0],
            primal_weight[0, 0],
            coarse_group[0],
            coarse_map[0],
            coarse_top,
            load_vector[0, 0],
            previous[0, 0],
            slot_count,
            partner[0, 0],
            face_size[0, 0],
        )
        return sol[None, None], res[None, None]

    both = ("wide", "narrow")
    deep = P(*both, None, None, None, None)
    return jax.shard_map(
        body,
        mesh=mesh,
        in_specs=(
            P(*both, None, None, None),
            deep,
            deep,
            P(*both, None, None, None),
            P(*both, None),
            P(*both, None),
            P("wide", None),
            deep,
            deep,
            P(*both),
            P(*both, None, None),
            P(*both, None, None),
        ),
        out_specs=(deep, deep),
        check_vma=False,
    )
```

time: 347 us -> 95.9 us (0.28); the launches traced: 343 us -> 95.7 us
  blocking collectives: 126 us -> 0 us
  Pallas kernels: 0 us -> 87.8 us
  starting transfers between devices: 84 us -> 0 us
  waiting for transfers between devices: 44.2 us -> 0 us
  local copies, waits for them, and re-layouts: 40.8 us -> 6.62 us
  matrix products: 25.5 us -> 0 us
  other arithmetic: 19.7 us -> 0 us
    psum x12 -> x0, blocking collectives: 99.5 us -> none  [over_axes(): shard = lax.psum(shard, axis)]
    pallas_call x0 -> x1, Pallas kernels: none -> 87.8 us  [body(): pl.pallas_call(functools.partial(kernel, wide, narrow), out_shape=[jax.Sh...]
    ppermute x24 -> x0, starting transfers between devices: 53.9 us -> none  [the longest x12 30.2 us: with_halo(): lax.ppermute(lax.slice_in_dim(block, 0, width, axis=dim), axis, backward)]
    all_to_all x4 -> x0, starting transfers between devices: 30.1 us -> none  [copy_for_each(): return lax.all_to_all(copies, axis, split_axis=0, concat_axis=0, tiled=True)]
    all_to_all x4 -> x0, waiting for transfers between devices: 29.9 us -> none  [copy_for_each(): return lax.all_to_all(copies, axis, split_axis=0, concat_axis=0, tiled=True)]
    all_to_all x2 -> x0, blocking collectives: 26.7 us -> none  [copy_for_each(): return lax.all_to_all(copies, axis, split_axis=0, concat_axis=0, tiled=True)]
    dot_general x15 -> x0, matrix products: 25.5 us -> none  [the longest x3 13.4 us: operator(): jnp.einsum('sij,sjr->sir', schur_matrix, stacked, preferred_element_type=...]
    unnamed x141 -> x6, local copies, waits for them, and re-layouts: 22.9 us -> 6.62 us
  transfers between devices with their start and end apart: 28 -> 0, of which waited for: 12 -> 0; matrix products, arithmetic and copies ran while one was open for 5% -> 0% of each run, Pallas kernels for 0% -> 0%
where the time goes in v1:
time: 95.9 us; the launch traced here: 95.7 us
  Pallas kernels  87.8 us (92%)
  local copies, waits for them, and re-layouts  6.62 us (7%)
  between operations  1.29 us (1%)
    pallas_call x1, Pallas kernels, body(): pl.pallas_call(functools.partial(kernel, wide, narrow), out_shape=[jax.Sh...  87.8 us
    unnamed x6, local copies, waits for them, and re-layouts  6.62 us

profile of v1, /device:TPU:1, one launch (start us, length us, event | category | flops | bytes accessed | tf_op | source)
XLA Modules:
  0.0 95.7 jit_solution(17775854566784300464)
XLA Ops:
  1.3 1.3 %copy_bitcast_fusion = (s32[3,8]{1,0:T(4,128)}, s32[3,8]{1,0:T(4,128)}) fusion(s32[1,1,3,8]{3,1,2,0:T(1,128)} %param.23, s32[1,1,3,8]{3,1,2,0:T(1,128)} %param.22), kind=kLoop, calls=%fused_computation | loop fusion | bytes 384
  2.6 1.4 %copy.14 = f32[1,24,8]{2,1,0:T(8,128)} copy(f32[1,24,8]{1,2,0:T(8,128)} %param.17) | data formatting | bytes 1536 | tf_op args[5]
  3.9 87.8 %shard_map.131 = (f32[3,8,128,128]{3,2,1,0:T(8,128)}, f32[3,8,128,128]{3,2,1,0:T(8,128)}) custom-call(bf16[3,1024,1024]{2,1,0:T(8,128)(2,1)} %bitcast.14, bf16[3,8,128,128]{3,2,1,0:T(8,128)(2,1)} %bitcast.17, bf16[3,8,128,128]{3,2,1,0:T(8,128)(2,1)} %bitcast.18, f32[3,8,128]{2,1,0:T(8,128)} %bitcast.23, f32[24,192]{1,0:T(8,128)} %bitcast.22, ...), custom_call_target="tpu_custom_call" | custom-call | tf_op jit(solution)/shard_map/pallas_call | solution.py:497
  91.8 0.0 copy-start
  91.8 2.8 %copy.22 = f32[1,1,3,8,128,128]{5,4,3,2,1,0:T(8,128)} copy(f32[1,1,3,8,128,128]{5,4,3,2,1,0:T(8,128)} %bitcast.16) | data formatting | bytes 3145728
  94.6 0.0 copy-done
  94.6 1.1 %copy.23 = f32[1,1,3,8,128,128]{5,4,3,2,1,0:T(8,128)} copy(f32[1,1,3,8,128,128]{5,4,3,2,1,0:T(8,128)S(1)} %bitcast.15) | data formatting | bytes 3145728
Async XLA Ops:
  91.8 2.8 %copy-start = (f32[3,8,128,128]{3,2,1,0:T(8,128)S(1)}, f32[3,8,128,128]{3,2,1,0:T(8,128)}, u32[]{:S(2)}) copy-start(f32[3,8,128,128]{3,2,1,0:T(8,128)} %get-tuple-element.5) | copy-start | bytes 4718596

commit v2 on v1

--- a/solution.py
+++ b/solution.py
@@ -16,7 +16,7 @@
 HIGH = lax.Precision.HIGHEST
 F32 = jnp.float32
 BF16 = jnp.bfloat16
-EXCHANGES = 2 * ITERS + 1
+EXCHANGES = ITERS + 1
 REDUCES = 2 * ITERS - 1
 
 
@@ -35,8 +35,11 @@
     count_ref,
     partner_ref,
     size_ref,
-    solution_out,
-    residual_out,
+    sol,
+    direc,
+    res,
+    full,
+    step_out,
     schur,
     inverse,
     deluxe,
@@ -44,21 +47,29 @@
     previous,
     turned,
     weight,
-    sol,
-    res,
-    direc,
     image,
     weighted,
     local,
+    lift,
+    over_deluxe,
+    over_inverse,
+    over_turned,
+    over_weight,
+    over_local,
     half,
     scaled_half,
     coarse,
+    group,
+    third,
+    top_buf,
     got_half,
     got_0,
     got_1,
     got_2,
-    got_3,
-    got_4,
+    rows_out,
+    rows_0,
+    rows_1,
+    rows_2,
     vec_buf,
     part_buf,
     every_buf,
@@ -79,9 +90,15 @@
     plane_recv,
     line_send,
     line_recv,
-    out_sem,
+    top_send,
+    top_recv,
+    over_send,
+    over_recv,
+    rows_send,
+    rows_recv,
 ):
-    got = (got_0, got_1, got_2, got_3, got_4)
+    got = (got_0, got_1, got_2)
+    rows_got = (rows_0, rows_1, rows_2)
     w = lax.axis_index("wide")
     n = lax.axis_index("narrow")
 
@@ -116,14 +133,14 @@
     count = count_ref[0, 0]
 
     def inside(s, f):
-        size = jnp.where(s < count, size_ref[s, f], 0)
+        size = jnp.where(s < count, size_ref[s, 0, f], 0)
         return rows < size
 
     def masked(s, f, values):
         return jnp.where(inside(s, f), values, 0.0)
 
     def picked(values, arrived, s, f):
-        t = partner_ref[s, f]
+        t = partner_ref[s, 0, f]
         slot = jnp.maximum(t, 0)
         source = arrived[f, slot] if f < 4 else values[slot, f ^ 1]
         return jnp.where(t >= 0, source.astype(F32), 0.0)
@@ -160,6 +177,41 @@
         right.start()
         left.start()
 
+    def send_rows(i, row_of):
+        for to, f in ((0, 1), (1, 0), (2, 3), (3, 2)):
+            rows_out[i, to] = jnp.concatenate(
+                [row_of(s, f) for s in range(SLOTS)] + [jnp.zeros((8 - SLOTS, FW), F32)], axis=0
+            )
+        up, down, right, left = [
+            pltpu.make_async_remote_copy(
+                src_ref=rows_out.at[i, to],
+                dst_ref=rows_got[i].at[to],
+                send_sem=rows_send.at[i, to],
+                recv_sem=rows_recv.at[i, to],
+                device_id=device,
+                device_id_type=MESH,
+            )
+            for to, device in enumerate(
+                (
+                    (w, lax.rem(n + 1, narrow)),
+                    (w, lax.rem(n + narrow - 1, narrow)),
+                    (lax.rem(w + 1, wide), n),
+                    (lax.rem(w + wide - 1, wide), n),
+                )
+            )
+        ]
+
+        @pl.when(n < narrow - 1)
+        def _():
+            up.start()
+
+        @pl.when(n > 0)
+        def _():
+            down.start()
+
+        right.start()
+        left.start()
+
     def wait_bytes(ref, sem):
         pltpu.make_async_copy(ref, ref, sem).wait()
 
@@ -258,13 +310,21 @@
 
     for s in range(SLOTS):
         send_faces(previous, got_half, half_send, half_recv, s)
+    send_rows(ITERS, lambda s, f: weight_in[s, f : f + 1, :])
+    for s in range(SLOTS):
+        send_faces(deluxe, over_deluxe, over_send.at[0], over_recv.at[0], s)
+    loads[4].wait()
+    for s in range(SLOTS):
+        send_faces(inverse, over_inverse, over_send.at[1], over_recv.at[1], s)
+    top_buf[w] = top_ref[...]
+    spread_wide(top_buf, top_send, top_recv)
     wait_faces(got_half, half_recv)
 
     def average(s, carry):
         for f in range(NF):
             own = previous[s, f].astype(F32)
             across = picked(previous, got_half, s, f)
-            mean = jnp.where(partner_ref[s, f] >= 0, 0.5 * (own + across), own)
+            mean = jnp.where(partner_ref[s, 0, f] >= 0, 0.5 * (own + across), own)
             mean = masked(s, f, mean)
             sol[s, f] = mean
             half[s, pl.ds(f * FW, FW), :] = mean.astype(BF16)
@@ -284,47 +344,118 @@
         return carry
 
     lax.fori_loop(0, SLOTS, start_residual, 0)
-    loads[4].wait()
     zero = jnp.zeros((8, FW), F32)
 
-    def scaled_of(m, s, f, values):
+    def scaled_of(s, f, values):
         scaled = masked(
             s, f, jnp.dot(turned[s, f], values.astype(BF16), preferred_element_type=F32)
         )
         scaled_half[s, f] = scaled.astype(BF16)
-        return jnp.sum(fold(weight[s, f] * scaled), axis=0, keepdims=True)
+        return scaled
+
+    def column_sum(values):
+        return jnp.sum(values, axis=0, keepdims=True)
 
     def coarse_start(m):
         entering = vec_buf[m, n]
-        part_buf[m, n] = lax.dot_general(
-            map_ref[...], entering, (((0,), (0,)), ((), ())), precision=HIGH
-        )
+        part_buf[m, n] = jnp.dot(map_ref[...], entering, precision=HIGH)
         spread_narrow(part_buf.at[m], part_send.at[m], part_recv.at[m])
         spread_narrow(vec_buf.at[m], vec_send.at[m], vec_recv.at[m])
 
     def local_parts():
+        def one(s, total):
+            for f in range(NF):
+                entering = scaled_half[s, f]
+                value = masked(
+                    s, f, jnp.dot(inverse[s, f], entering, preferred_element_type=F32)
+                )
+                local[s, f] = value
+                total = total + fold(entering.astype(F32) * value)
+            return total
+
+        return lax.fori_loop(0, SLOTS, one, zero)
+
+    def over_tables(s, carry):
+        for f in range(4):
+            slot = jnp.maximum(partner_ref[s, 0, f], 0)
+            over_turned[s, f] = over_deluxe[f, slot].T
+            row = rows_2[f, pl.ds(slot, 1), :]
+            over_weight[s, f] = masked(s, f, jnp.broadcast_to(row, (FW, FW)).T)
+        return carry
+
+    def over_parts():
         def one(s, carry):
-            for f in range(NF):
-                local[s, f] = masked(
-                    s, f, jnp.dot(inverse[s, f], scaled_half[s, f], preferred_element_type=F32)
+            for f in range(4):
+                slot = jnp.maximum(partner_ref[s, 0, f], 0)
+                scaled = masked(
+                    s,
+                    f,
+                    jnp.dot(
+                        over_turned[s, f], res[s, f].astype(BF16), preferred_element_type=F32
+                    ),
+                )
+                over_local[s, f] = masked(
+                    s,
+                    f,
+                    jnp.dot(
+                        over_inverse[f, slot], scaled.astype(BF16), preferred_element_type=F32
+                    ),
                 )
             return carry
 
         lax.fori_loop(0, SLOTS, one, 0)
 
-    def coarse_end(m):
+    def across_weighted(m, s, f):
+        t = partner_ref[s, 0, f]
+        slot = jnp.maximum(t, 0)
+        if f < 4:
+            out = rows_got[m][f, pl.ds(slot, 1), :]
+            correction = (over_local[s, f] + over_weight[s, f] * out).astype(BF16)
+            value = masked(
+                s, f, jnp.dot(over_deluxe[f, slot], correction, preferred_element_type=F32)
+            )
+        else:
+            value = weighted[slot, f ^ 1]
+        return jnp.where(t >= 0, value, 0.0)
+
+    def coarse_row(s, f):
+        return coarse[s * NF + f : s * NF + f + 1, :]
+
+    def wait_rows(i):
+        wait_faces(rows_got[i], rows_recv.at[i])
+
+    def make_lift(s, carry):
+        for f in range(NF):
+            value = weight[s, f]
+            main = value.astype(BF16)
+            rest = (value - main.astype(F32)).astype(BF16)
+            lift[s, f] = jnp.dot(deluxe[s, f], main, preferred_element_type=F32) + jnp.dot(
+                deluxe[s, f], rest, preferred_element_type=F32
+            )
+        return carry
+
+    def coarse_middle(m):
         wait_spread(part_buf.at[m], part_recv.at[m])
         every_buf[m, w] = jnp.sum(part_buf[m], axis=0)
         spread_wide(every_buf.at[m], every_send.at[m], every_recv.at[m])
         wait_spread(vec_buf.at[m], vec_recv.at[m])
-        group = jnp.dot(
+        group[m] = jnp.dot(
             group_ref[...], vec_buf[m].reshape(narrow * SLOTS * NF, FW), precision=HIGH
         )
+
+    def coarse_end(m):
         wait_spread(every_buf.at[m], every_recv.at[m])
-        top = jnp.dot(top_ref[...], every_buf[m].reshape(wide * 8, FW), precision=HIGH)
-        coarse[...] = group + jnp.dot(map_ref[...], top, precision=HIGH)
-
-    def weigh(e, send_now):
+        third[m] = jnp.dot(
+            top_buf[...].reshape(wide * 8, wide * 8),
+            every_buf[m].reshape(wide * 8, FW),
+            precision=HIGH,
+        )
+        own = third[m, pl.ds(pl.multiple_of(w * 8, 8), 8), :]
+        return group[m] + lax.dot_general(
+            map_ref[...], own, (((0,), (0,)), ((), ())), precision=HIGH
+        )
+
+    def weigh():
         def one(s, total):
             for f in range(NF):
                 out = coarse[pl.ds(s * NF + f, 1), :]
@@ -334,13 +465,11 @@
                 )
                 weighted[s, f] = value
                 total = total + fold(res[s, f] * value)
-            if send_now:
-                send_faces(weighted, got[e], face_send.at[e], face_recv.at[e], s)
             return total
 
         return lax.fori_loop(0, SLOTS, one, zero)
 
-    def operate(e):
+    def operate():
         def one(s, total):
             product = jnp.dot(schur[s], half[s], preferred_element_type=F32)
             for f in range(NF):
@@ -365,47 +494,68 @@
         for f in range(NF):
             value = image[s, f] + picked(image, got[0], s, f)
             res[s, f] = value
-            primal.append(scaled_of(0, s, f, value))
+            primal.append(column_sum(fold(weight[s, f] * scaled_of(s, f, value))))
         vec_buf[0, n, pl.ds(s * NF, NF), :] = jnp.concatenate(primal, axis=0)
         return carry
 
     lax.fori_loop(0, SLOTS, first_residual, 0)
     coarse_start(0)
     local_parts()
-    coarse_end(0)
-    norm_part = weigh(1, True)
-    wait_faces(got[1], face_recv.at[1])
+    lax.fori_loop(0, SLOTS, make_lift, 0)
+    wait_rows(ITERS)
+    wait_faces(over_deluxe, over_recv.at[0])
+    wait_faces(over_inverse, over_recv.at[1])
+    lax.fori_loop(0, SLOTS, over_tables, 0)
+    coarse_middle(0)
+    over_parts()
+    wait_spread(top_buf, top_recv)
+    coarse[...] = coarse_end(0)
+    send_rows(0, coarse_row)
+    norm_part = weigh()
+    wait_rows(0)
 
     def first_direction(s, carry):
         for f in range(NF):
-            value = weighted[s, f] + picked(weighted, got[1], s, f)
+            value = weighted[s, f] + across_weighted(0, s, f)
             direc[s, f] = value
             half[s, pl.ds(f * FW, FW), :] = value.astype(BF16)
         return carry
 
     lax.fori_loop(0, SLOTS, first_direction, 0)
     wait_sent(got[0], face_send.at[0])
-    curve_part = operate(2)
+    curve_part = operate()
     reduce_start(0, norm_part, curve_part)
-    send_all(image, 2)
+    send_all(image, 1)
     reduce_middle(0)
-    wait_faces(got[2], face_recv.at[2])
+    wait_faces(got[1], face_recv.at[1])
+
+    def full_image(s, carry):
+        primal = []
+        for f in range(NF):
+            value = image[s, f] + picked(image, got[1], s, f)
+            full[s, f] = value
+            primal.append(column_sum(fold(lift[s, f] * value)))
+        vec_buf[1, n, pl.ds(s * NF, NF), :] = jnp.concatenate(primal, axis=0)
+        return carry
+
+    lax.fori_loop(0, SLOTS, full_image, 0)
+    coarse_start(1)
     norm, curve = reduce_end(0)
     step = norm / curve
 
     def next_residual(s, carry):
-        primal = []
-        for f in range(NF):
-            full = image[s, f] + picked(image, got[2], s, f)
-            value = res[s, f] - step * full
+        for f in range(NF):
+            value = res[s, f] - step * full[s, f]
             res[s, f] = value
-            primal.append(scaled_of(1, s, f, value))
-        vec_buf[1, n, pl.ds(s * NF, NF), :] = jnp.concatenate(primal, axis=0)
+            scaled_of(s, f, value)
         return carry
 
     lax.fori_loop(0, SLOTS, next_residual, 0)
-    coarse_start(1)
-    local_parts()
+    norm_part = local_parts()
+    coarse_middle(1)
+    second = (vec_buf[0, n] - step * vec_buf[1, n]) * (group[0] - step * group[1])
+    norm_part = norm_part + (second[0:8] + second[8:16] + second[16:24])
+    reduce_start(1, norm_part, norm_part)
 
     def next_solution(s, carry):
         for f in range(NF):
@@ -413,54 +563,48 @@
         return carry
 
     lax.fori_loop(0, SLOTS, next_solution, 0)
-    wait_sent(got[1], face_send.at[1])
-    coarse_end(1)
-    norm_part = weigh(3, False)
-    reduce_start(1, norm_part, norm_part)
-    send_all(weighted, 3)
+    over_parts()
+    coarse[...] = coarse[...] - step * coarse_end(1)
+    send_rows(1, coarse_row)
     reduce_middle(1)
-    wait_faces(got[3], face_recv.at[3])
+    weigh()
+    entered = (every_buf[0] - step * every_buf[1]).reshape(wide * 8, FW)
+    third_norm = column_sum(entered * (third[0] - step * third[1]))
+    wait_rows(1)
     following, _ = reduce_end(1)
+    following = following + third_norm
     ratio = following / norm
 
     def next_direction(s, carry):
         for f in range(NF):
-            value = weighted[s, f] + picked(weighted, got[3], s, f)
+            value = weighted[s, f] + across_weighted(1, s, f)
             value = value + ratio * direc[s, f]
             direc[s, f] = value
             half[s, pl.ds(f * FW, FW), :] = value.astype(BF16)
         return carry
 
     lax.fori_loop(0, SLOTS, next_direction, 0)
-    wait_sent(got[2], face_send.at[2])
-    curve_part = operate(4)
+    wait_sent(got[1], face_send.at[1])
+    curve_part = operate()
     reduce_start(2, curve_part, curve_part)
-    send_all(image, 4)
+    send_all(image, 2)
     reduce_middle(2)
-    wait_faces(got[4], face_recv.at[4])
+    wait_faces(got[2], face_recv.at[2])
 
     def last_image(s, carry):
         for f in range(NF):
-            local[s, f] = image[s, f] + picked(image, got[4], s, f)
+            full[s, f] = image[s, f] + picked(image, got[2], s, f)
         return carry
 
     lax.fori_loop(0, SLOTS, last_image, 0)
     curve, _ = reduce_end(2)
-    step = following / curve
-    outs = []
-    for s in range(SLOTS):
-        for f in range(NF):
-            sol[s, f] = sol[s, f] + step * direc[s, f]
-        outs.append(pltpu.make_async_copy(sol.at[s], solution_out.at[s], out_sem.at[0, s]))
-        outs[-1].start()
-        for f in range(NF):
-            res[s, f] = res[s, f] - step * local[s, f]
-        outs.append(pltpu.make_async_copy(res.at[s], residual_out.at[s], out_sem.at[1, s]))
-        outs[-1].start()
-
+    step_out[...] = following / curve
     wait_sent(got_half, half_send)
-    wait_sent(got[3], face_send.at[3])
-    wait_sent(got[4], face_send.at[4])
+    wait_sent(got[2], face_send.at[2])
+    wait_sent(over_deluxe, over_send.at[0])
+    wait_sent(over_inverse, over_send.at[1])
+    for i in range(ITERS + 1):
+        wait_sent(rows_got[i], rows_send.at[i])
     for m in range(ITERS):
         wait_spread(part_buf.at[m], part_send.at[m])
         wait_spread(vec_buf.at[m], vec_send.at[m])
@@ -468,8 +612,7 @@
     for k in range(REDUCES):
         wait_spread(plane_buf.at[k], plane_send.at[k])
         wait_spread(line_buf.at[k], line_send.at[k])
-    for copy in outs:
-        copy.wait()
+    wait_spread(top_buf, top_send)
 
 
 def solution(mesh):
@@ -491,14 +634,14 @@
         partner,
         face_size,
     ):
-        far = pl.BlockSpec(memory_space=pl.ANY)
+        far = pl.BlockSpec(memory_space=pltpu.HBM)
         near = pl.BlockSpec(memory_space=pltpu.VMEM)
         scalar = pl.BlockSpec(memory_space=pltpu.SMEM)
-        sol, res = pl.pallas_call(
+        sol, direc, res, image, step = pl.pallas_call(
             functools.partial(kernel, wide, narrow),
-            out_shape=[jax.ShapeDtypeStruct(faces, F32)] * 2,
+            out_shape=[pltpu.VMEM(faces, F32)] * 4 + [pltpu.VMEM((1, FW), F32)],
             in_specs=[far, far, far, near, near, near, near, far, far, scalar, scalar, scalar],
-            out_specs=[far, far],
+            out_specs=[near] * 5,
             scratch_shapes=[
                 pltpu.VMEM((SLOTS, NB, NB), BF16),
                 pltpu.VMEM(faces, BF16),
@@ -511,13 +654,21 @@
                 pltpu.VMEM(faces, F32),
                 pltpu.VMEM(faces, F32),
                 pltpu.VMEM(faces, F32),
-                pltpu.VMEM(faces, F32),
-                pltpu.VMEM(faces, F32),
+                pltpu.VMEM((4, SLOTS, FW, FW), BF16),
+                pltpu.VMEM((4, SLOTS, FW, FW), BF16),
+                pltpu.VMEM((SLOTS, 4, FW, FW), BF16),
+                pltpu.VMEM((SLOTS, 4, FW, FW), F32),
+                pltpu.VMEM((SLOTS, 4, FW, FW), F32),
                 pltpu.VMEM((SLOTS, NB, FW), BF16),
                 pltpu.VMEM(faces, BF16),
                 pltpu.VMEM((SLOTS * NF, FW), F32),
+                pltpu.VMEM((ITERS, SLOTS * NF, FW), F32),
+                pltpu.VMEM((ITERS, wide * 8, FW), F32),
+                pltpu.VMEM((wide, 8, wide * 8), F32),
                 pltpu.VMEM((4, SLOTS, FW, FW), BF16),
                 *[pltpu.VMEM((4, SLOTS, FW, FW), F32)] * EXCHANGES,
+                pltpu.VMEM((ITERS + 1, 4, 8, FW), F32),
+                *[pltpu.VMEM((4, 8, FW), F32)] * (ITERS + 1),
                 pltpu.VMEM((ITERS, narrow, SLOTS * NF, FW), F32),
                 pltpu.VMEM((ITERS, narrow, 8, FW), F32),
                 pltpu.VMEM((ITERS, wide, 8, FW), F32),
@@ -538,10 +689,15 @@
                 dma((REDUCES,)),
                 dma((REDUCES,)),
                 dma((REDUCES,)),
-                dma((2, SLOTS)),
+                dma(()),
+                dma(()),
+                dma((2, 4)),
+                dma((2, 4)),
+                dma((ITERS + 1, 4)),
+                dma((ITERS + 1, 4)),
             ],
             compiler_params=pltpu.CompilerParams(
-                collective_id=0, has_side_effects=True, vmem_limit_bytes=60 * 1024 * 1024
+                collective_id=0, has_side_effects=True, vmem_limit_bytes=58880 * 1024
             ),
         )(
             schur_matrix[0, 0],
@@ -549,15 +705,15 @@
             deluxe[0, 0],
             primal_weight[0, 0],
             coarse_group[0],
-            coarse_map[0],
+            coarse_map[0].T,
             coarse_top,
             load_vector[0, 0],
             previous[0, 0],
             slot_count,
-            partner[0, 0],
-            face_size[0, 0],
+            partner.reshape(SLOTS, 1, NF),
+            face_size.reshape(SLOTS, 1, NF),
         )
-        return sol[None, None], res[None, None]
+        return (sol + step * direc)[None, None], (res - step * image)[None, None]
 
     both = ("wide", "narrow")
     deep = P(*both, None, None, None, None)

time: 95.9 us -> 80.9 us (0.84)
  Pallas kernels: 87.8 us -> 77 us
  local copies, waits for them, and re-layouts: 6.62 us -> 0 us
  other arithmetic: 0 us -> 2.48 us
    pallas_call x1, Pallas kernels: 87.8 us -> 77 us  [body(): pl.pallas_call(functools.partial(kernel, wide, narrow), out_shape=[pltpu....]
    unnamed x6 -> x0, local copies, waits for them, and re-layouts: 6.62 us -> none
    broadcast_in_dim x0 -> x1, other arithmetic: none -> 2.48 us  [body(): return ((sol + step * direc)[None, None], (res - step * image)[None, None])]
where the time goes in v2:
time: 80.9 us; the launch traced here: 80.8 us
  Pallas kernels  77 us (95%)
  other arithmetic  2.48 us (3%)
  between operations  1.29 us (2%)
    pallas_call x1, Pallas kernels, body(): pl.pallas_call(functools.partial(kernel, wide, narrow), out_shape=[pltpu....  77 us
    broadcast_in_dim x1, other arithmetic, body(): return ((sol + step * direc)[None, None], (res - step * image)[None, None])  2.48 us

profile of v2, /device:TPU:1, one launch (start us, length us, event | category | flops | bytes accessed | tf_op | source)
XLA Modules:
  0.0 80.8 jit_solution(1205852269390040619)
XLA Ops:
  1.3 77.0 %shard_map.131 = (f32[3,8,128,128]{3,2,1,0:T(8,128)S(1)}, f32[3,8,128,128]{3,2,1,0:T(8,128)S(1)}, f32[3,8,128,128]{3,2,1,0:T(8,128)S(1)}, f32[3,8,128,128]{3,2,1,0:T(8,128)S(1)}, f32[1,128]{1,0:T(1,128)S(1)}) custom-call(bf16[3,1024,1024]{2,1,0:T(8,128)(2,1)} %bitcast.18, bf16[3,8,128,128]{3,2,1,0:T(8,128)(2,1)} %bitcast.19, ...), custom_call_target="tpu_custom_call" | custom-call | tf_op jit(solution)/shard_map/pallas_call | solution.py:640
  78.3 2.5 %subtract_bitcast_fusion = (f32[1,1,3,8,128,128]{5,4,3,2,1,0:T(8,128)}, f32[1,1,3,8,128,128]{5,4,3,2,1,0:T(8,128)}) fusion(f32[3,8,128,128]{3,2,1,0:T(8,128)S(1)} %get-tuple-element.10, f32[3,8,128,128]{3,2,1,0:T(8,128)S(1)} %get-tuple-element.11, f32[128]{0:T(128)S(1)} %bitcast.17, f32[3,8,128,128]{3,2,1,0:T(8,128)S(1)} %get-tuple-element.7, ...), kind=kLoop, calls=%fused_computation | loop fusion | flops 1572864 | bytes 9437696 | tf_op jit(solution)/shard_map/broadcast_in_dim | solution.py:716

commit v3 on v2

--- a/solution.py
+++ b/solution.py
@@ -51,6 +51,7 @@
     weighted,
     local,
     lift,
+    ahead,
     over_deluxe,
     over_inverse,
     over_turned,
@@ -145,44 +146,44 @@
         source = arrived[f, slot] if f < 4 else values[slot, f ^ 1]
         return jnp.where(t >= 0, source.astype(F32), 0.0)
 
-    def face_copies(values, arrived, send, recv, s):
-        return [
-            pltpu.make_async_remote_copy(
-                src_ref=values.at[s, f],
-                dst_ref=arrived.at[to, s],
-                send_sem=send.at[to],
-                recv_sem=recv.at[to],
-                device_id=device,
-                device_id_type=MESH,
-            )
-            for f, to, device in (
-                (1, 0, (w, lax.rem(n + 1, narrow))),
-                (0, 1, (w, lax.rem(n + narrow - 1, narrow))),
-                (3, 2, (lax.rem(w + 1, wide), n)),
-                (2, 3, (lax.rem(w + wide - 1, wide), n)),
-            )
-        ]
-
-    def send_faces(values, arrived, send, recv, s):
-        up, down, right, left = face_copies(values, arrived, send, recv, s)
-
+    above = (w, lax.rem(n + 1, narrow))
+    below = (w, lax.rem(n + narrow - 1, narrow))
+    right = (lax.rem(w + 1, wide), n)
+    left = (lax.rem(w + wide - 1, wide), n)
+
+    def send_face(values, arrived, send, recv, s, f, to, device):
+        pltpu.make_async_remote_copy(
+            src_ref=values.at[s, f],
+            dst_ref=arrived.at[to, s],
+            send_sem=send.at[to],
+            recv_sem=recv.at[to],
+            device_id=device,
+            device_id_type=MESH,
+        ).start()
+
+    def send_narrow(values, arrived, send, recv, s):
         @pl.when(n < narrow - 1)
         def _():
-            up.start()
+            send_face(values, arrived, send, recv, s, 1, 0, above)
 
         @pl.when(n > 0)
         def _():
-            down.start()
-
-        right.start()
-        left.start()
+            send_face(values, arrived, send, recv, s, 0, 1, below)
+
+    def send_wide(values, arrived, send, recv, s):
+        send_face(values, arrived, send, recv, s, 3, 2, right)
+        send_face(values, arrived, send, recv, s, 2, 3, left)
+
+    def send_faces(values, arrived, send, recv, s):
+        send_narrow(values, arrived, send, recv, s)
+        send_wide(values, arrived, send, recv, s)
 
     def send_rows(i, row_of):
         for to, f in ((0, 1), (1, 0), (2, 3), (3, 2)):
             rows_out[i, to] = jnp.concatenate(
                 [row_of(s, f) for s in range(SLOTS)] + [jnp.zeros((8 - SLOTS, FW), F32)], axis=0
             )
-        up, down, right, left = [
+        to_above, to_below, to_right, to_left = [
             pltpu.make_async_remote_copy(
                 src_ref=rows_out.at[i, to],
                 dst_ref=rows_got[i].at[to],
@@ -191,26 +192,19 @@
                 device_id=device,
                 device_id_type=MESH,
             )
-            for to, device in enumerate(
-                (
-                    (w, lax.rem(n + 1, narrow)),
-                    (w, lax.rem(n + narrow - 1, narrow)),
-                    (lax.rem(w + 1, wide), n),
-                    (lax.rem(w + wide - 1, wide), n),
-                )
-            )
+            for to, device in enumerate((above, below, right, left))
         ]
 
         @pl.when(n < narrow - 1)
         def _():
-            up.start()
+            to_above.start()
 
         @pl.when(n > 0)
         def _():
-            down.start()
-
-        right.start()
-        left.start()
+            to_below.start()
+
+        to_right.start()
+        to_left.start()
 
     def wait_bytes(ref, sem):
         pltpu.make_async_copy(ref, ref, sem).wait()
@@ -254,7 +248,7 @@
         lax.fori_loop(1, narrow, one, 0)
 
     def spread_wide(buf, send, recv):
-        def one(d, carry):
+        def one(d):
             pltpu.make_async_remote_copy(
                 src_ref=buf.at[w],
                 dst_ref=buf.at[w],
@@ -263,9 +257,15 @@
                 device_id=(lax.rem(w + d, wide), n),
                 device_id_type=MESH,
             ).start()
+
+        def four(i, carry):
+            for d in range(4):
+                one(4 * i + d)
             return carry
 
-        lax.fori_loop(1, wide, one, 0)
+        for d in range(1, 4):
+            one(d)
+        lax.fori_loop(1, wide // 4, four, 0)
 
     def wait_spread(buf, sem):
         wait_bytes(buf.at[pl.ds(0, buf.shape[0] - 1)], sem)
@@ -318,24 +318,40 @@
         send_faces(inverse, over_inverse, over_send.at[1], over_recv.at[1], s)
     top_buf[w] = top_ref[...]
     spread_wide(top_buf, top_send, top_recv)
+
+    def average(faces):
+        def one(s, carry):
+            for f in faces:
+                own = previous[s, f].astype(F32)
+                across = picked(previous, got_half, s, f)
+                mean = jnp.where(partner_ref[s, 0, f] >= 0, 0.5 * (own + across), own)
+                mean = masked(s, f, mean)
+                sol[s, f] = mean
+                half[s, pl.ds(f * FW, FW), :] = mean.astype(BF16)
+            return carry
+
+        lax.fori_loop(0, SLOTS, one, 0)
+
+    def go_ahead(s, carry):
+        ahead[s] = jnp.dot(
+            schur[s, :, NB // 2 :], half[s, pl.ds(NB // 2, NB // 2), :], preferred_element_type=F32
+        )
+        return carry
+
+    def rest_of_product(s):
+        return ahead[s] + jnp.dot(
+            schur[s, :, : NB // 2], half[s, pl.ds(0, NB // 2), :], preferred_element_type=F32
+        )
+
+    average(range(4, NF))
+    loads[2].wait()
+    lax.fori_loop(0, SLOTS, go_ahead, 0)
     wait_faces(got_half, half_recv)
-
-    def average(s, carry):
-        for f in range(NF):
-            own = previous[s, f].astype(F32)
-            across = picked(previous, got_half, s, f)
-            mean = jnp.where(partner_ref[s, 0, f] >= 0, 0.5 * (own + across), own)
-            mean = masked(s, f, mean)
-            sol[s, f] = mean
-            half[s, pl.ds(f * FW, FW), :] = mean.astype(BF16)
-        return carry
-
-    lax.fori_loop(0, SLOTS, average, 0)
-    loads[2].wait()
+    average(range(4))
     loads[3].wait()
 
     def start_residual(s, carry):
-        product = jnp.dot(schur[s], half[s], preferred_element_type=F32)
+        product = rest_of_product(s)
         for f in range(NF):
             image[s, f] = masked(
                 s, f, load[s, f].astype(F32) - product[f * FW : (f + 1) * FW]
@@ -469,20 +485,24 @@
 
         return lax.fori_loop(0, SLOTS, one, zero)
 
-    def operate():
+    def operate(e, begun):
         def one(s, total):
-            product = jnp.dot(schur[s], half[s], preferred_element_type=F32)
+            if begun:
+                product = rest_of_product(s)
+            else:
+                product = jnp.dot(schur[s], half[s], preferred_element_type=F32)
             for f in range(NF):
                 value = masked(s, f, product[f * FW : (f + 1) * FW])
                 image[s, f] = value
                 total = total + fold(direc[s, f] * value)
+            send_narrow(image, got[e], face_send.at[e], face_recv.at[e], s)
             return total
 
         return lax.fori_loop(0, SLOTS, one, zero)
 
-    def send_all(values, e):
+    def send_sideways(e):
         def one(s, carry):
-            send_faces(values, got[e], face_send.at[e], face_recv.at[e], s)
+            send_wide(image, got[e], face_send.at[e], face_recv.at[e], s)
             return carry
 
         lax.fori_loop(0, SLOTS, one, 0)
@@ -512,20 +532,25 @@
     coarse[...] = coarse_end(0)
     send_rows(0, coarse_row)
     norm_part = weigh()
+
+    def first_direction(faces):
+        def one(s, carry):
+            for f in faces:
+                value = weighted[s, f] + across_weighted(0, s, f)
+                direc[s, f] = value
+                half[s, pl.ds(f * FW, FW), :] = value.astype(BF16)
+            return carry
+
+        lax.fori_loop(0, SLOTS, one, 0)
+
+    first_direction(range(4, NF))
+    lax.fori_loop(0, SLOTS, go_ahead, 0)
     wait_rows(0)
-
-    def first_direction(s, carry):
-        for f in range(NF):
-            value = weighted[s, f] + across_weighted(0, s, f)
-            direc[s, f] = value
-            half[s, pl.ds(f * FW, FW), :] = value.astype(BF16)
-        return carry
-
-    lax.fori_loop(0, SLOTS, first_direction, 0)
+    first_direction(range(4))
     wait_sent(got[0], face_send.at[0])
-    curve_part = operate()
+    curve_part = operate(1, True)
     reduce_start(0, norm_part, curve_part)
-    send_all(image, 1)
+    send_sideways(1)
     reduce_middle(0)
     wait_faces(got[1], face_recv.at[1])
 
@@ -585,9 +610,9 @@
 
     lax.fori_loop(0, SLOTS, next_direction, 0)
     wait_sent(got[1], face_send.at[1])
-    curve_part = operate()
+    curve_part = operate(2, False)
     reduce_start(2, curve_part, curve_part)
-    send_all(image, 2)
+    send_sideways(2)
     reduce_middle(2)
     wait_faces(got[2], face_recv.at[2])
 
@@ -640,7 +665,7 @@
         sol, direc, res, image, step = pl.pallas_call(
             functools.partial(kernel, wide, narrow),
             out_shape=[pltpu.VMEM(faces, F32)] * 4 + [pltpu.VMEM((1, FW), F32)],
-            in_specs=[far, far, far, near, near, near, near, far, far, scalar, scalar, scalar],
+            in_specs=[far, far, far, near, near, near, near, far, far, near, scalar, scalar],
             out_specs=[near] * 5,
             scratch_shapes=[
                 pltpu.VMEM((SLOTS, NB, NB), BF16),
@@ -654,6 +679,7 @@
                 pltpu.VMEM(faces, F32),
                 pltpu.VMEM(faces, F32),
                 pltpu.VMEM(faces, F32),
+                pltpu.VMEM((SLOTS, NB, FW), F32),
                 pltpu.VMEM((4, SLOTS, FW, FW), BF16),
                 pltpu.VMEM((4, SLOTS, FW, FW), BF16),
                 pltpu.VMEM((SLOTS, 4, FW, FW), BF16),

time: 80.9 us -> 79.3 us (0.980)
  Pallas kernels: 77 us -> 75.3 us
    pallas_call x1, Pallas kernels: 77 us -> 75.3 us  [body(): pl.pallas_call(functools.partial(kernel, wide, narrow), out_shape=[pltpu....]
where the time goes in v3:
time: 79.3 us; the launch traced here: 79.1 us
  Pallas kernels  75.3 us (95%)
  other arithmetic  2.48 us (3%)
  between operations  1.29 us (2%)
    pallas_call x1, Pallas kernels, body(): pl.pallas_call(functools.partial(kernel, wide, narrow), out_shape=[pltpu....  75.3 us
    broadcast_in_dim x1, other arithmetic, body(): return ((sol + step * direc)[None, None], (res - step * image)[None, None])  2.48 us

profile of v3, /device:TPU:1, one launch (start us, length us, event | category | flops | bytes accessed | tf_op | source)
XLA Modules:
  0.0 79.1 jit_solution(7986017821807211560)
XLA Ops:
  1.3 75.3 %shard_map.131 = (f32[3,8,128,128]{3,2,1,0:T(8,128)S(1)}, f32[3,8,128,128]{3,2,1,0:T(8,128)S(1)}, f32[3,8,128,128]{3,2,1,0:T(8,128)S(1)}, f32[3,8,128,128]{3,2,1,0:T(8,128)S(1)}, f32[1,128]{1,0:T(1,128)S(1)}) custom-call(bf16[3,1024,1024]{2,1,0:T(8,128)(2,1)} %bitcast.18, bf16[3,8,128,128]{3,2,1,0:T(8,128)(2,1)} %bitcast.19, ...), custom_call_target="tpu_custom_call" | custom-call | tf_op jit(solution)/shard_map/pallas_call | solution.py:665
  76.6 2.5 %subtract_bitcast_fusion = (f32[1,1,3,8,128,128]{5,4,3,2,1,0:T(8,128)}, f32[1,1,3,8,128,128]{5,4,3,2,1,0:T(8,128)}) fusion(f32[3,8,128,128]{3,2,1,0:T(8,128)S(1)} %get-tuple-element.10, f32[3,8,128,128]{3,2,1,0:T(8,128)S(1)} %get-tuple-element.11, f32[128]{0:T(128)S(1)} %bitcast.17, f32[3,8,128,128]{3,2,1,0:T(8,128)S(1)} %get-tuple-element.7, ...), kind=kLoop, calls=%fused_computation | loop fusion | flops 1572864 | bytes 9437696 | tf_op jit(solution)/shard_map/broadcast_in_dim | solution.py:742
